TPU v7x, 32 devices: a whole 2x2x4 slice. The times are simulated.
32 devices in a mesh: fluid: 8 (over y, x, core), solid: 4 (over z).
Axes of the slice: x: 2, y: 2, z: 4, core: 2. Of those that a mesh axis runs over, the one named last changes fastest.
Arguments:
- earlier_thermal_state: float32 [256, 128, 128], P('fluid', 'solid'), may hold values from -6 to 6
- thermal_inertia: float32 [256, 128, 128], P('fluid', 'solid'), may hold values from 0.3 to 3
- boundary_energy_current: float32 [64, 16384], P(None, ('fluid', 'solid')), may hold values from -6 to 6
- jacobian_quad_factors: float32 [64, 32768], P(None, ('fluid', 'solid')), may hold values from 0.05 to 0.4
- patch_holder_liquid: int32 [32768, 1], P(('fluid', 'solid')), may hold values from 0 to 7; in each aligned block of 1024 rows (0 to 1023, 1024 to 2047, ...) at most 512 rows name the same one
- patch_slot_number: int32 [32768], P(('fluid', 'solid')), may hold values from 0 to 511
Outputs:
- thermal_state_guess: float32 [256, 128, 128], P('fluid', 'solid')
- equation_misfit: float32 [256, 128, 128], P('fluid', 'solid')
Inputs may be any that keep to these rules, and one draw needn't show every extreme that they name: `patch_holder_liquid`: within the rows of one device, no owner index is named by more than 512 rows; in the rows of some device one owner index is named by exactly 512 rows.
All inputs are finite; a program needn't handle non-finite values.
Results may differ from a plain program's by a relative error of at most 0.00025.
Values sent between devices are 32-bit elements; how exact they have to be, the bound alone decides.
No kernel may reach another device: no remote copies, remote signals or barrier semaphores. Data moves between devices by JAX's collectives and lax.ppermute only.
A program may use at most 64 MiB of HBM per device.

v0:
```python
import jax
import jax.numpy as jnp
from jax import lax
from jax.sharding import PartitionSpec as P

ITERS = 3


def extended(shard, sides, width):
    for axis, dim in sides:
        size, length = (lax.axis_size(axis), shard.shape[dim])
        up = [(i, (i + 1) % size) for i in range(size - 1)]
        down = [(j, i) for i, j in up]
        last = lax.slice_in_dim(shard, length - width, length, axis=dim)
        initial = lax.slice_in_dim(shard, 0, width, axis=dim)
        before = lax.ppermute(last, axis, up)
        after = lax.ppermute(initial, axis, down)
        shard = jnp.concatenate([before, shard, after], axis=dim)
    return shard


def matrix_action(field, thermal_inertia):
    padded = extended(field, (("fluid", 0), ("solid", 1)), 1)
    padded = jnp.pad(padded, ((0, 0), (0, 0), (1, 1)))
    beside = padded[2:, 1:-1, 1:-1] + padded[:-2, 1:-1, 1:-1]
    beside = beside + padded[1:-1, 2:, 1:-1] + padded[1:-1, :-2, 1:-1]
    beside = beside + padded[1:-1, 1:-1, 2:] + padded[1:-1, 1:-1, :-2]
    return (6.0 + thermal_inertia) * field - beside


def paired_sums(equation_misfit, precond, image):
    return lax.psum(
        (jnp.sum(equation_misfit * precond), jnp.sum(image * precond)), ("fluid", "solid")
    )


def per_device(
    earlier_thermal_state,
    thermal_inertia,
    boundary_energy_current,
    jacobian_quad_factors,
    patch_holder_liquid,
    patch_slot_number,
):
    owner_index = patch_holder_liquid[:, 0]
    gathered = lax.all_gather(boundary_energy_current, "fluid", axis=1, tiled=True)
    columns = owner_index * boundary_energy_current.shape[1] + patch_slot_number
    picked = jnp.take(gathered, columns, axis=1)
    source = jnp.sum(jacobian_quad_factors * picked, axis=0).reshape(
        earlier_thermal_state.shape[0], earlier_thermal_state.shape[1]
    )
    forcing_entries = thermal_inertia * earlier_thermal_state
    forcing_entries = forcing_entries.at[:, :, -1].add(source)
    diagonal = 6.0 + thermal_inertia
    thermal_state_guess = earlier_thermal_state
    equation_misfit = forcing_entries - matrix_action(thermal_state_guess, thermal_inertia)
    precond = equation_misfit / diagonal
    image = matrix_action(precond, thermal_inertia)
    norm_now, product = paired_sums(equation_misfit, precond, image)
    update_multiplier = norm_now / product
    update_course = precond
    along = image
    for iteration in range(ITERS):
        thermal_state_guess = thermal_state_guess + update_multiplier * update_course
        equation_misfit = equation_misfit - update_multiplier * along
        if iteration + 1 < ITERS:
            precond = equation_misfit / diagonal
            image = matrix_action(precond, thermal_inertia)
            norm_next, product = paired_sums(equation_misfit, precond, image)
            ratio = norm_next / norm_now
            update_multiplier = norm_next / (product - ratio * norm_next / update_multiplier)
            update_course = precond + ratio * update_course
            along = image + ratio * along
            norm_now = norm_next
    return (thermal_state_guess, equation_misfit)


def solution(mesh):
    return jax.shard_map(
        per_device,
        mesh=mesh,
        in_specs=(
            P("fluid", "solid", None),
            P("fluid", "solid", None),
            P(None, ("fluid", "solid")),
            P(None, ("fluid", "solid")),
            P(("fluid", "solid"), None),
            P(("fluid", "solid")),
        ),
        out_specs=(P("fluid", "solid", None), P("fluid", "solid", None)),
        check_vma=False,
    )
```

profile of v0, /device:TPU:0, one launch (start us, length us, event | category | flops | bytes accessed | tf_op | source)
XLA Modules:
  0.0 248.4 jit_solution(11429353709327466096)
XLA Ops:
  7.2 0.0 all-gather.2.cloned.1.call-start
  7.2 1.7 copy.158
  9.0 0.0 all-gather.2.cloned.1.call-update
  9.0 0.8 fusion.27
  9.8 1.3 collective-permute-start
  11.0 3.0 %collective-permute-start.1 = (f32[1,32,128]{2,1,0:T(8,128)S(1)}, f32[1,32,128]{2,1,0:T(8,128)S(1)}, u32[]{:S(2)}, u32[]{:S(2)}) collective-permute-start(f32[1,32,128]{2,1,0:T(8,128)S(1)} %get-tuple-element.58), channel_id=1, source_target_pairs={{0,4},{4,8},{8,12},{12,16},{16,20},{20,24},{24,28},{1,5},{5,9},{9,... | collective-permute-start | bytes 49160 | tf_op jit(solution)/shard_map/ppermute | solution.py:16
  14.1 0.7 broadcast_multiply_fusion
  14.8 0.7 broadcast_clamp_fusion
  15.5 0.0 collective-permute-done.1
  15.5 1.3 constant_dynamic-update-slice_fusion.1
  16.8 0.0 collective-permute-done
  16.8 5.0 %collective-permute-start.3 = (f32[34,1,128]{2,1,0:T(1,128)S(1)}, f32[34,1,128]{2,1,0:T(1,128)S(1)}, u32[]{:S(2)}, u32[]{:S(2)}) collective-permute-start(f32[34,1,128]{2,1,0:T(1,128)S(1)} %get-tuple-element.49), channel_id=1, source_target_pairs={{0,1},{1,2},{2,3},{4,5},{5,6},{6,7},{8,9},{9,10},{10,11},{12,13},{... | collective-permute-start | bytes 52232 | tf_op jit(solution)/shard_map/ppermute | solution.py:16
  21.8 1.3 collective-permute-start.2
  23.1 0.2 copy.159
  23.3 0.0 collective-permute-done.3
  23.4 4.1 %collective-permute-done.2 = f32[34,1,128]{2,1,0:T(1,128)S(1)} collective-permute-done((f32[34,1,128]{2,1,0:T(1,128)S(1)}, f32[34,1,128]{2,1,0:T(1,128)S(1)}, u32[]{:S(2)}, u32[]{:S(2)}) %collective-permute-start.2) | collective-permute-done | bytes 17440 | tf_op jit(solution)/shard_map/ppermute | solution.py:17
  27.5 1.7 select_maximum_fusion.12
  29.2 11.8 %all-gather.2.cloned.1.call-done = f32[64,4096]{0,1:T(8,128)} async-done(((f32[64,512]{0,1:T(8,128)}), f32[64,4096]{0,1:T(8,128)}) %all-gather.2.cloned.1.call-update) | async-done | bytes 1048592 | tf_op jit(solution)/shard_map/all_gather | solution.py:46
  41.0 4.4 %gather_fusion = f32[1024,64]{1,0:T(8,128)S(1)} fusion(f32[64,4096]{0,1:T(8,128)} %all-gather.2.cloned.1.call-done, s32[1024]{0:T(1024)S(1)} %broadcast_clamp_fusion), kind=kCustom, calls=%fused_computation | custom fusion | bytes 528384 | tf_op jit(solution)/shard_map/jit(_take)/gather | solution.py:48
  45.4 0.4 fusion.18
  45.7 0.3 reshape.54
  46.1 0.0 copy-start
  46.1 0.0 copy-start.1
  46.1 0.2 slice_add_fusion.8
  46.3 3.0 %scatter-add.4 = f32[32,32,128]{2,1,0:T(8,128)S(1)} dynamic-update-slice(f32[32,32,128]{2,1,0:T(8,128)S(1)} %get-tuple-element.60, f32[32,32,1]{2,1,0:T(8,128)S(1)} %slice_add_fusion.8, s32[]{:T(128)} %constant.45.clone.1, s32[]{:T(128)} %constant.45.clone.1, s32[]{:T(128)} %constant.50.clone.1) | dynamic-update-slice | bytes 8196 | tf_op jit(solution)/shard_map/scatter-add | solution.py:53
  49.4 2.2 add_divide_fusion.2
  51.6 2.1 collective-permute-start.5
  53.8 1.3 collective-permute-start.4
  55.1 0.0 collective-permute-done.5
  55.1 2.6 %collective-permute-done.4 = f32[1,32,128]{2,1,0:T(8,128)S(1)} collective-permute-done((f32[1,32,128]{2,1,0:T(8,128)S(1)}, f32[1,32,128]{2,1,0:T(8,128)S(1)}, u32[]{:S(2)}, u32[]{:S(2)}) %collective-permute-start.4) | collective-permute-done | bytes 16416 | tf_op jit(solution)/shard_map/ppermute | solution.py:17
  57.7 3.4 %collective-permute-start.7 = (f32[34,1,128]{2,1,0:T(1,128)S(1)}, f32[34,1,128]{2,1,0:T(1,128)S(1)}, u32[]{:S(2)}, u32[]{:S(2)}) collective-permute-start(f32[34,1,128]{2,1,0:T(1,128)S(1)} %get-tuple-element.47), channel_id=1, source_target_pairs={{0,1},{1,2},{2,3},{4,5},{5,6},{6,7},{8,9},{9,10},{10,11},{12,13},{... | collective-permute-start | bytes 52232 | tf_op jit(solution)/shard_map/ppermute | solution.py:16
  61.1 1.3 collective-permute-start.6
  62.4 0.1 collective-permute-done.7
  62.6 4.2 %collective-permute-done.6 = f32[34,1,128]{2,1,0:T(1,128)S(1)} collective-permute-done((f32[34,1,128]{2,1,0:T(1,128)S(1)}, f32[34,1,128]{2,1,0:T(1,128)S(1)}, u32[]{:S(2)}, u32[]{:S(2)}) %collective-permute-start.6) | collective-permute-done | bytes 17440 | tf_op jit(solution)/shard_map/ppermute | solution.py:17
  66.8 0.6 select_maximum_fusion.8
  67.4 1.1 multiply_reduce_fusion.4
  68.5 40.9 %all-reduce.6 = (f32[]{:T(128)}, f32[]{:T(128)}) all-reduce(f32[]{:T(128)} %get-tuple-element.27, f32[]{:T(128)} %get-tuple-element.26), channel_id=1, replica_groups=mesh['fluid'=8,'solid'=4] {'fluid','solid'}, use_global_device_ids=true, to_apply=%region_2.3 | all-reduce | flops 2 | bytes 16 | tf_op jit(solution)/shard_map/psum | solution.py:32
  110.6 0.2 add_divide_fusion.1
  110.8 0.0 copy-start.3
  110.8 1.3 collective-permute-start.9
  112.1 1.3 collective-permute-start.8
  113.4 0.0 collective-permute-done.9
  113.4 4.3 %collective-permute-done.8 = f32[1,32,128]{2,1,0:T(8,128)S(1)} collective-permute-done((f32[1,32,128]{2,1,0:T(8,128)S(1)}, f32[1,32,128]{2,1,0:T(8,128)S(1)}, u32[]{:S(2)}, u32[]{:S(2)}) %collective-permute-start.8) | collective-permute-done | bytes 16416 | tf_op jit(solution)/shard_map/ppermute | solution.py:17
  117.7 2.3 collective-permute-start.11
  120.1 1.3 collective-permute-start.10
  121.4 0.1 collective-permute-done.11
  121.5 4.2 %collective-permute-done.10 = f32[34,1,128]{2,1,0:T(1,128)S(1)} collective-permute-done((f32[34,1,128]{2,1,0:T(1,128)S(1)}, f32[34,1,128]{2,1,0:T(1,128)S(1)}, u32[]{:S(2)}, u32[]{:S(2)}) %collective-permute-start.10) | collective-permute-done | bytes 17440 | tf_op jit(solution)/shard_map/ppermute | solution.py:17
  125.7 0.6 select_maximum_fusion.4
  126.3 2.0 multiply_reduce_fusion.2
  128.3 42.0 %all-reduce.5 = (f32[]{:T(128)}, f32[]{:T(128)}) all-reduce(f32[]{:T(128)} %get-tuple-element.25, f32[]{:T(128)} %get-tuple-element.24), channel_id=1, replica_groups=mesh['fluid'=8,'solid'=4] {'fluid','solid'}, use_global_device_ids=true, to_apply=%region_6.7 | all-reduce | flops 2 | bytes 16 | tf_op jit(solution)/shard_map/psum | solution.py:32
  174.7 1.4 add_divide_fusion
  176.1 0.0 copy-start.2
  176.1 1.3 collective-permute-start.13
  177.4 1.3 collective-permute-start.12
  178.7 0.0 collective-permute-done.13
  178.7 4.3 %collective-permute-done.12 = f32[1,32,128]{2,1,0:T(8,128)S(1)} collective-permute-done((f32[1,32,128]{2,1,0:T(8,128)S(1)}, f32[1,32,128]{2,1,0:T(8,128)S(1)}, u32[]{:S(2)}, u32[]{:S(2)}) %collective-permute-start.12) | collective-permute-done | bytes 16416 | tf_op jit(solution)/shard_map/ppermute | solution.py:17
  183.1 2.4 collective-permute-start.15
  185.4 1.3 collective-permute-start.14
  186.7 0.1 collective-permute-done.15
  186.9 4.2 %collective-permute-done.14 = f32[34,1,128]{2,1,0:T(1,128)S(1)} collective-permute-done((f32[34,1,128]{2,1,0:T(1,128)S(1)}, f32[34,1,128]{2,1,0:T(1,128)S(1)}, u32[]{:S(2)}, u32[]{:S(2)}) %collective-permute-start.14) | collective-permute-done | bytes 17440 | tf_op jit(solution)/shard_map/ppermute | solution.py:17
  191.1 0.6 select_maximum_fusion
  191.7 1.9 multiply_reduce_fusion
  193.6 41.2 %all-reduce.4 = (f32[]{:T(128)}, f32[]{:T(128)}) all-reduce(f32[]{:T(128)} %get-tuple-element.23, f32[]{:T(128)} %get-tuple-element.22), channel_id=1, replica_groups=mesh['fluid'=8,'solid'=4] {'fluid','solid'}, use_global_device_ids=true, to_apply=%region_10.11 | all-reduce | flops 2 | bytes 16 | tf_op jit(solution)/shard_map/psum | solution.py:32
  238.7 2.8 %multiply_subtract_fusion = (f32[32,32,128]{2,1,0:T(8,128)}, f32[32,32,128]{2,1,0:T(8,128)}) fusion(f32[32,32,128]{2,1,0:T(8,128)} %copy-done.2, f32[32,32,128]{2,1,0:T(8,128)} %get-tuple-element.34, f32[]{:T(128)S(6)} %div.37, f32[]{:T(128)S(6)} %div.39, f32[32,32,128]{2,1,0:T(8,128)} %get-tuple-element.37, f32[32,32,128]{2,1,0:T(8,128)S(1)} %get-tuple-element.40, ...), kind=kLoop, calls=%fused_computation.74 | loop fusion | flops 2097152 | bytes 5242900 | tf_op jit(solution)/shard_map/sub | solution.py:65
  (20 shorter events, 0.2 us)
Async XLA Ops:
  7.2 33.8 %all-gather.2.cloned.1.call-start = ((), (), s32[]{:S(2)}) async-start(), calls=%async_computation | async-start | bytes 2359296 | tf_op jit(solution)/shard_map/all_gather | solution.py:46
  8.9 14.2 %copy-start.6 = (s32[1024]{0:T(1024)S(1)}, s32[1024]{0:T(1024)}, u32[]{:S(2)}) copy-start(s32[1024]{0:T(1024)} %param.13) | copy-start | bytes 12292
  9.0 14.2 %copy-start.5 = (f32[64,1024]{1,0:T(8,128)S(1)}, f32[64,1024]{1,0:T(8,128)}, u32[]{:S(2)}) copy-start(f32[64,1024]{1,0:T(8,128)} %param.11) | copy-start | bytes 786436
  9.8 7.0 %collective-permute-start = (f32[1,32,128]{2,1,0:T(8,128)S(1)}, f32[1,32,128]{2,1,0:T(8,128)S(1)}, u32[]{:S(2)}, u32[]{:S(2)}) collective-permute-start(f32[1,32,128]{2,1,0:T(8,128)S(1)} %get-tuple-element.57), channel_id=1, source_target_pairs={{4,0},{8,4},{12,8},{16,12},{20,16},{24,20},{28,24},{5,1},{9,5},{13... | collective-permute-start | bytes 49160 | tf_op jit(solution)/shard_map/ppermute | solution.py:17
  11.0 4.4 %collective-permute-start.1 = (f32[1,32,128]{2,1,0:T(8,128)S(1)}, f32[1,32,128]{2,1,0:T(8,128)S(1)}, u32[]{:S(2)}, u32[]{:S(2)}) collective-permute-start(f32[1,32,128]{2,1,0:T(8,128)S(1)} %get-tuple-element.58), channel_id=1, source_target_pairs={{0,4},{4,8},{8,12},{12,16},{16,20},{20,24},{24,28},{1,5},{5,9},{9,... | collective-permute-start | bytes 49160 | tf_op jit(solution)/shard_map/ppermute | solution.py:16
  16.8 12.4 %copy-start.4 = (f32[34,32,128]{2,1,0:T(8,128)}, f32[34,32,128]{2,1,0:T(8,128)S(1)}, u32[]{:S(2)}) copy-start(f32[34,32,128]{2,1,0:T(8,128)S(1)} %constant_dynamic-update-slice_fusion) | copy-start | bytes 1671172
  16.8 6.5 %collective-permute-start.3 = (f32[34,1,128]{2,1,0:T(1,128)S(1)}, f32[34,1,128]{2,1,0:T(1,128)S(1)}, u32[]{:S(2)}, u32[]{:S(2)}) collective-permute-start(f32[34,1,128]{2,1,0:T(1,128)S(1)} %get-tuple-element.49), channel_id=1, source_target_pairs={{0,1},{1,2},{2,3},{4,5},{5,6},{6,7},{8,9},{9,10},{10,11},{12,13},{... | collective-permute-start | bytes 52232 | tf_op jit(solution)/shard_map/ppermute | solution.py:16
  21.8 5.7 %collective-permute-start.2 = (f32[34,1,128]{2,1,0:T(1,128)S(1)}, f32[34,1,128]{2,1,0:T(1,128)S(1)}, u32[]{:S(2)}, u32[]{:S(2)}) collective-permute-start(f32[34,1,128]{2,1,0:T(1,128)S(1)} %get-tuple-element.50), channel_id=1, source_target_pairs={{1,0},{2,1},{3,2},{5,4},{6,5},{7,6},{9,8},{10,9},{11,10},{13,12},{... | collective-permute-start | bytes 52232 | tf_op jit(solution)/shard_map/ppermute | solution.py:17
  46.1 3.3 %copy-start = (f32[32,32,128]{2,1,0:T(8,128)S(1)}, f32[32,32,128]{2,1,0:T(8,128)}, u32[]{:S(2)}) copy-start(f32[32,32,128]{2,1,0:T(8,128)} %param.9) | copy-start | bytes 1572868
  46.1 3.3 %copy-start.1 = (f32[32,32,128]{2,1,0:T(8,128)S(1)}, f32[32,32,128]{2,1,0:T(8,128)}, u32[]{:S(2)}) copy-start(f32[32,32,128]{2,1,0:T(8,128)} %param.8) | copy-start | bytes 1572868
  51.6 3.5 %collective-permute-start.5 = (f32[1,32,128]{2,1,0:T(8,128)S(1)}, f32[1,32,128]{2,1,0:T(8,128)S(1)}, u32[]{:S(2)}, u32[]{:S(2)}) collective-permute-start(f32[1,32,128]{2,1,0:T(8,128)S(1)} %get-tuple-element.55), channel_id=1, source_target_pairs={{0,4},{4,8},{8,12},{12,16},{16,20},{20,24},{24,28},{1,5},{5,9},{9,... | collective-permute-start | bytes 49160 | tf_op jit(solution)/shard_map/ppermute | solution.py:16
  53.8 3.9 %collective-permute-start.4 = (f32[1,32,128]{2,1,0:T(8,128)S(1)}, f32[1,32,128]{2,1,0:T(8,128)S(1)}, u32[]{:S(2)}, u32[]{:S(2)}) collective-permute-start(f32[1,32,128]{2,1,0:T(8,128)S(1)} %get-tuple-element.56), channel_id=1, source_target_pairs={{4,0},{8,4},{12,8},{16,12},{20,16},{24,20},{28,24},{5,1},{9,5},{13... | collective-permute-start | bytes 49160 | tf_op jit(solution)/shard_map/ppermute | solution.py:17
  57.7 4.8 %collective-permute-start.7 = (f32[34,1,128]{2,1,0:T(1,128)S(1)}, f32[34,1,128]{2,1,0:T(1,128)S(1)}, u32[]{:S(2)}, u32[]{:S(2)}) collective-permute-start(f32[34,1,128]{2,1,0:T(1,128)S(1)} %get-tuple-element.47), channel_id=1, source_target_pairs={{0,1},{1,2},{2,3},{4,5},{5,6},{6,7},{8,9},{9,10},{10,11},{12,13},{... | collective-permute-start | bytes 52232 | tf_op jit(solution)/shard_map/ppermute | solution.py:16
  61.1 5.6 %collective-permute-start.6 = (f32[34,1,128]{2,1,0:T(1,128)S(1)}, f32[34,1,128]{2,1,0:T(1,128)S(1)}, u32[]{:S(2)}, u32[]{:S(2)}) collective-permute-start(f32[34,1,128]{2,1,0:T(1,128)S(1)} %get-tuple-element.48), channel_id=1, source_target_pairs={{1,0},{2,1},{3,2},{5,4},{6,5},{7,6},{9,8},{10,9},{11,10},{13,12},{... | collective-permute-start | bytes 52232 | tf_op jit(solution)/shard_map/ppermute | solution.py:17
  110.8 17.5 %copy-start.3 = (f32[32,32,128]{2,1,0:T(8,128)}, f32[32,32,128]{2,1,0:T(8,128)S(1)}, u32[]{:S(2)}) copy-start(f32[32,32,128]{2,1,0:T(8,128)S(1)} %get-tuple-element.39) | copy-start | bytes 1572868
  110.8 2.6 %collective-permute-start.9 = (f32[1,32,128]{2,1,0:T(8,128)S(1)}, f32[1,32,128]{2,1,0:T(8,128)S(1)}, u32[]{:S(2)}, u32[]{:S(2)}) collective-permute-start(f32[1,32,128]{2,1,0:T(8,128)S(1)} %get-tuple-element.53), channel_id=1, source_target_pairs={{0,4},{4,8},{8,12},{12,16},{16,20},{20,24},{24,28},{1,5},{5,9},{9,... | collective-permute-start | bytes 49160 | tf_op jit(solution)/shard_map/ppermute | solution.py:16
  112.1 5.6 %collective-permute-start.8 = (f32[1,32,128]{2,1,0:T(8,128)S(1)}, f32[1,32,128]{2,1,0:T(8,128)S(1)}, u32[]{:S(2)}, u32[]{:S(2)}) collective-permute-start(f32[1,32,128]{2,1,0:T(8,128)S(1)} %get-tuple-element.54), channel_id=1, source_target_pairs={{4,0},{8,4},{12,8},{16,12},{20,16},{24,20},{28,24},{5,1},{9,5},{13... | collective-permute-start | bytes 49160 | tf_op jit(solution)/shard_map/ppermute | solution.py:17
  117.7 3.8 %collective-permute-start.11 = (f32[34,1,128]{2,1,0:T(1,128)S(1)}, f32[34,1,128]{2,1,0:T(1,128)S(1)}, u32[]{:S(2)}, u32[]{:S(2)}) collective-permute-start(f32[34,1,128]{2,1,0:T(1,128)S(1)} %get-tuple-element.45), channel_id=1, source_target_pairs={{0,1},{1,2},{2,3},{4,5},{5,6},{6,7},{8,9},{9,10},{10,11},{12,13},{... | collective-permute-start | bytes 52232 | tf_op jit(solution)/shard_map/ppermute | solution.py:16
  120.1 5.6 %collective-permute-start.10 = (f32[34,1,128]{2,1,0:T(1,128)S(1)}, f32[34,1,128]{2,1,0:T(1,128)S(1)}, u32[]{:S(2)}, u32[]{:S(2)}) collective-permute-start(f32[34,1,128]{2,1,0:T(1,128)S(1)} %get-tuple-element.46), channel_id=1, source_target_pairs={{1,0},{2,1},{3,2},{5,4},{6,5},{7,6},{9,8},{10,9},{11,10},{13,12},{... | collective-permute-start | bytes 52232 | tf_op jit(solution)/shard_map/ppermute | solution.py:17
  176.1 17.5 %copy-start.2 = (f32[32,32,128]{2,1,0:T(8,128)}, f32[32,32,128]{2,1,0:T(8,128)S(1)}, u32[]{:S(2)}) copy-start(f32[32,32,128]{2,1,0:T(8,128)S(1)} %get-tuple-element.36) | copy-start | bytes 1572868
  176.1 2.6 %collective-permute-start.13 = (f32[1,32,128]{2,1,0:T(8,128)S(1)}, f32[1,32,128]{2,1,0:T(8,128)S(1)}, u32[]{:S(2)}, u32[]{:S(2)}) collective-permute-start(f32[1,32,128]{2,1,0:T(8,128)S(1)} %get-tuple-element.51), channel_id=1, source_target_pairs={{0,4},{4,8},{8,12},{12,16},{16,20},{20,24},{24,28},{1,5},{5,9},{9,... | collective-permute-start | bytes 49160 | tf_op jit(solution)/shard_map/ppermute | solution.py:16
  177.4 5.6 %collective-permute-start.12 = (f32[1,32,128]{2,1,0:T(8,128)S(1)}, f32[1,32,128]{2,1,0:T(8,128)S(1)}, u32[]{:S(2)}, u32[]{:S(2)}) collective-permute-start(f32[1,32,128]{2,1,0:T(8,128)S(1)} %get-tuple-element.52), channel_id=1, source_target_pairs={{4,0},{8,4},{12,8},{16,12},{20,16},{24,20},{28,24},{5,1},{9,5},{13... | collective-permute-start | bytes 49160 | tf_op jit(solution)/shard_map/ppermute | solution.py:17
  183.1 3.8 %collective-permute-start.15 = (f32[34,1,128]{2,1,0:T(1,128)S(1)}, f32[34,1,128]{2,1,0:T(1,128)S(1)}, u32[]{:S(2)}, u32[]{:S(2)}) collective-permute-start(f32[34,1,128]{2,1,0:T(1,128)S(1)} %get-tuple-element.43), channel_id=1, source_target_pairs={{0,1},{1,2},{2,3},{4,5},{5,6},{6,7},{8,9},{9,10},{10,11},{12,13},{... | collective-permute-start | bytes 52232 | tf_op jit(solution)/shard_map/ppermute | solution.py:16
  185.4 5.6 %collective-permute-start.14 = (f32[34,1,128]{2,1,0:T(1,128)S(1)}, f32[34,1,128]{2,1,0:T(1,128)S(1)}, u32[]{:S(2)}, u32[]{:S(2)}) collective-permute-start(f32[34,1,128]{2,1,0:T(1,128)S(1)} %get-tuple-element.44), channel_id=1, source_target_pairs={{1,0},{2,1},{3,2},{5,4},{6,5},{7,6},{9,8},{10,9},{11,10},{13,12},{... | collective-permute-start | bytes 52232 | tf_op jit(solution)/shard_map/ppermute | solution.py:17
Sparse Core Ops, SparseCore 0:
  10.4 30.4 all-gather.1
where the time goes:
time: 250 us; the launch traced here: 248 us
  blocking collectives  124 us (50%)
  waiting for transfers between devices  40.2 us (16%)
  starting transfers between devices  31.2 us (12%)
  between operations  24 us (10%)
  other arithmetic  18.4 us (7%)
  local copies, waits for them, and re-layouts  10.6 us (4%)
    psum x3, blocking collectives, paired_sums(): lax.psum((jnp.sum(equation_misfit * precond), jnp.sum(image * precond)),...  124 us
    ppermute x8, waiting for transfers between devices, extended(): after = lax.ppermute(initial, axis, down)  28 us
    ppermute x8, starting transfers between devices, extended(): before = lax.ppermute(last, axis, up)  20.8 us
    all_gather x1, waiting for transfers between devices, per_device(): lax.all_gather(boundary_energy_current, 'fluid', axis=1, tiled=True)  11.8 us
    ppermute x8, starting transfers between devices, extended(): after = lax.ppermute(initial, axis, down)  10.3 us
  transfers between devices with their start and end apart: 17, of which 11 were waited for; matrix products, arithmetic and copies ran while one was open for 2% of the time, Pallas kernels for 0%

commit v1 on v0

v1 whole, which is shorter than its diff:
```python
import functools

import jax
import jax.numpy as jnp
from jax import lax
from jax.experimental import pallas as pl
from jax.experimental.pallas import tpu as pltpu
from jax.sharding import PartitionSpec as P

ITERS = 3
HALO = ITERS + 1
MOMENTS = 2 * ITERS
PAD = 8
BOTH = ("fluid", "solid")
VMEM = pl.BlockSpec(memory_space=pltpu.VMEM)
F32 = jnp.float32
BF16 = jnp.bfloat16


def params():
    return pltpu.CompilerParams(vmem_limit_bytes=24 * 1024 * 1024)


def cost(flops, size=0):
    return pl.CostEstimate(flops=flops, bytes_accessed=size, transcendentals=0)


def shift(axis, step):
    size = lax.axis_size(axis)
    if step > 0:
        return [(i, i + 1) for i in range(size - 1)]
    return [(i + 1, i) for i in range(size - 1)]


def edge_kernel(field, inertia, factors, slot, holder, head, tail):
    cx, cy, _ = field.shape
    edge = HALO * cy
    thick = (HALO - 1) * cy
    quads, rows = factors.shape
    spots = ((head, 0, 0, 0), (tail, cx - HALO, cx - HALO + 1, rows - edge))
    for out, field_at, inertia_at, row_at in spots:
        out[0:edge, :] = field[field_at : field_at + HALO].reshape(edge, -1)
        out[edge : edge + thick, :] = inertia[inertia_at : inertia_at + HALO - 1].reshape(thick, -1)
        top = edge + thick
        out[top : top + quads, :] = factors[:, row_at : row_at + edge]
        top = top + quads
        marks = jnp.concatenate(
            [
                slot[:, row_at : row_at + edge].astype(F32),
                holder[:, row_at : row_at + edge].astype(F32),
                jnp.zeros((6, edge), F32),
            ],
            axis=0,
        )
        out[top : top + 8, :] = marks


def edges(field, inertia, factors, slot, holder):
    cx, cy, cz = field.shape
    edge = HALO * cy
    length = edge + (HALO - 1) * cy + factors.shape[0] + 8
    shape = jax.ShapeDtypeStruct((length, cz), F32)
    return pl.pallas_call(
        edge_kernel,
        out_shape=(shape, shape),
        in_specs=[VMEM] * 5,
        out_specs=(VMEM, VMEM),
        compiler_params=params(),
        cost_estimate=cost(10**5),
        name="edges",
    )(field, inertia, factors, slot, holder)


def side_kernel(field, inertia, below, above, first, last):
    cx, cy, cz = field.shape
    edge = HALO * cy
    thin = HALO - 1
    thick = thin * cy
    for out, field_at, inertia_at in ((first, 0, 0), (last, cy - HALO, cy - thin)):
        for got, at, inertia_to in ((below, 0, 1), (above, cx + HALO, cx + HALO)):
            slab = got[0:edge, :].reshape(HALO, cy, cz)
            out[at : at + HALO, 0:HALO, :] = slab[:, field_at : field_at + HALO, :]
            slab = got[edge : edge + thick, :].reshape(thin, cy, cz)
            out[inertia_to : inertia_to + thin, HALO : HALO + thin, :] = slab[:, inertia_at : inertia_at + thin, :]
        out[HALO : HALO + cx, 0:HALO, :] = field[:, field_at : field_at + HALO, :]
        out[HALO : HALO + cx, HALO : HALO + thin, :] = inertia[:, inertia_at : inertia_at + thin, :]
        zero = jnp.zeros((1, thin, cz), F32)
        out[0:1, HALO : HALO + thin, :] = zero
        out[cx + 2 * HALO - 1 : cx + 2 * HALO, HALO : HALO + thin, :] = zero
        out[:, 2 * HALO - 1 : 2 * HALO, :] = jnp.zeros((cx + 2 * HALO, 1, cz), F32)


def sides(field, inertia, below, above):
    cx, cy, cz = field.shape
    shape = jax.ShapeDtypeStruct((cx + 2 * HALO, 2 * HALO, cz), F32)
    return pl.pallas_call(
        side_kernel,
        out_shape=(shape, shape),
        in_specs=[VMEM] * 4,
        out_specs=(VMEM, VMEM),
        compiler_params=params(),
        cost_estimate=cost(10**5),
        name="sides",
    )(field, inertia, below, above)


def source_kernel(count, cy, thick, *refs):
    blocks = refs[:count]
    factors, slot, holder, below, above, out, table, picked = refs[count:]
    quads, faces = blocks[0].shape
    rows = factors.shape[1]
    edge = HALO * cy
    top = edge + thick
    me = lax.axis_index("fluid")
    for k in range(count):
        value = blocks[k][...]
        high = value.astype(BF16)
        low = (value - high.astype(F32)).astype(BF16)
        table[2 * k * quads : (2 * k + 1) * quads, :] = high
        table[(2 * k + 1) * quads : (2 * k + 2) * quads, :] = low

    def part(slots, holders, weights, width):
        spot = lax.broadcasted_iota(jnp.int32, (faces, width), 0)
        chosen = jnp.where(spot == slots, 1.0, 0.0).astype(BF16)
        picked[:, 0:width] = jnp.dot(table[...], chosen, preferred_element_type=F32)
        total = jnp.zeros((quads, width), F32)
        for k in range(count):
            high = picked[2 * k * quads : (2 * k + 1) * quads, 0:width]
            low = picked[(2 * k + 1) * quads : (2 * k + 2) * quads, 0:width]
            total = total + jnp.where(holders == (me ^ k), high + low, 0.0)
        return jnp.sum(total * weights, axis=0, keepdims=True)

    def side(got):
        marks = got[top + quads : top + quads + 8, :]
        return marks[0:1, :].astype(jnp.int32), marks[1:2, :].astype(jnp.int32), got[top : top + quads, :]

    slots, holders, weights = (jnp.concatenate(t, axis=1) for t in zip(side(below), side(above)))
    both = part(slots, holders, weights, 2 * edge)
    out[:, 0:edge] = both[:, 0:edge]
    out[:, edge + rows : 2 * edge + rows] = both[:, edge : 2 * edge]
    width = 2 * edge
    for at in range(0, rows, width):
        spots = slice(at, at + width)
        out[:, edge + at : edge + at + width] = part(slot[:, spots], holder[:, spots], factors[:, spots], width)


def sources(blocks, factors, slot, holder, below, above, cy):
    count = len(blocks)
    quads, rows = factors.shape
    faces = blocks[0].shape[1]
    edge = HALO * cy
    return pl.pallas_call(
        functools.partial(source_kernel, count, cy, (HALO - 1) * cy),
        out_shape=jax.ShapeDtypeStruct((1, rows + 2 * edge), F32),
        in_specs=[VMEM] * (count + 5),
        out_specs=VMEM,
        scratch_shapes=[
            pltpu.VMEM((2 * quads * count, faces), BF16),
            pltpu.VMEM((2 * quads * count, 2 * edge), F32),
        ],
        compiler_params=params(),
        cost_estimate=cost(10**8),
        name="sources",
    )(*blocks, factors, slot, holder, below, above)


def neighbours(ref, at, wide):
    centre = ref[pl.ds(at, wide), :]
    lane = lax.broadcasted_iota(jnp.int32, centre.shape, 1)
    depth = centre.shape[1]
    lower = jnp.where(lane == 0, 0.0, pltpu.roll(centre, 1, 1))
    upper = jnp.where(lane == depth - 1, 0.0, pltpu.roll(centre, depth - 1, 1))
    total = ref[pl.ds(at - wide, wide), :] + ref[pl.ds(at + wide, wide), :]
    total = total + (ref[pl.ds(at - 1, wide), :] + ref[pl.ds(at + 1, wide), :])
    return centre, total + (lower + upper)


def widen_kernel(field, inertia, below, above, left, right, misfit, inverse, wide_field):
    cx, cy, cz = field.shape
    edge = HALO * cy
    thin = HALO - 1
    wide = cy + 2 * HALO
    tall = cx + 2 * HALO

    def row(x):
        return PAD + x * wide

    blank = jnp.zeros((PAD, cz), F32)
    for ref in (misfit, inverse, wide_field):
        ref[0:PAD, :] = blank
        ref[row(tall) : row(tall) + PAD, :] = blank
    for x in (0, tall - 1):
        misfit[row(x) : row(x + 1), :] = jnp.zeros((wide, cz), F32)
        inverse[row(x) : row(x + 1), :] = jnp.zeros((wide, cz), F32)

    def put(x, middle, capacity):
        start = row(x)
        if not isinstance(x, int):
            start = pl.multiple_of(start, 8)
        before, after = left[x], right[x]
        wide_field[pl.ds(start, wide), :] = jnp.concatenate([before[0:HALO], middle, after[0:HALO]], axis=0)
        if capacity is not None:
            none = jnp.zeros((1, cz), F32)
            full = jnp.concatenate(
                [none, before[HALO : HALO + thin], capacity, after[HALO : HALO + thin], none], axis=0
            )
            inverse[pl.ds(start, wide), :] = jnp.where(full > 0.0, 1.0 / (6.0 + full), 0.0)

    for x in range(HALO):
        at = edge + (x - 1) * cy
        put(x, below[x * cy : (x + 1) * cy, :], below[at : at + cy, :] if x > 0 else None)
        at = edge + x * cy
        put(
            cx + HALO + x,
            above[x * cy : (x + 1) * cy, :],
            above[at : at + cy, :] if x < thin else None,
        )

    def inner(x, carry):
        put(x + HALO, field[x], inertia[x])
        return carry

    lax.fori_loop(0, cx, inner, 0)

    def step(x, carry):
        at = pl.multiple_of(row(x), 8)
        centre, total = neighbours(wide_field, at, wide)
        misfit[pl.ds(at, wide), :] = total - 6.0 * centre
        return carry

    lax.fori_loop(1, tall - 1, step, 0)


def widen(field, inertia, below, above, left, right):
    cx, cy, cz = field.shape
    length = (cx + 2 * HALO) * (cy + 2 * HALO) + 2 * PAD
    shape = jax.ShapeDtypeStruct((length, cz), F32)
    return pl.pallas_call(
        widen_kernel,
        out_shape=(shape, shape),
        in_specs=[VMEM] * 6,
        out_specs=(VMEM, VMEM),
        scratch_shapes=[pltpu.VMEM((length, cz), F32)],
        compiler_params=params(),
        cost_estimate=cost(10**7),
        name="widen",
    )(field, inertia, below, above, left, right)


def basis_kernel(cx, cy, devices, misfit, inverse, inertia, own, left, right, *outs):
    basis, sums, spread = outs[: ITERS + 1], outs[ITERS + 1], outs[ITERS + 2]
    cz = misfit.shape[1]
    wide = cy + 2 * HALO
    tall = cx + 2 * HALO

    def row(x):
        return pl.multiple_of(PAD + x * wide, 8)

    rows = jnp.concatenate([own[...], left[...], right[...]], axis=0)
    high = rows.astype(BF16)
    rest = rows - high.astype(F32)
    mid = rest.astype(BF16)
    low = (rest - mid.astype(F32)).astype(BF16)
    stack = jnp.concatenate([high, mid, low], axis=0).astype(F32)
    index = lax.broadcasted_iota(jnp.int32, (9, cz), 0)
    lane9 = lax.broadcasted_iota(jnp.int32, (9, cz), 1)
    place = jnp.where(lane9 == cz - 1 - index % 3, 1.0, 0.0)
    spread[...] = lax.dot_general(
        stack.astype(BF16), place.astype(BF16), (((0,), (0,)), ((), ())), preferred_element_type=F32
    )

    def top(value, back):
        lane = lax.broadcasted_iota(jnp.int32, value.shape, 1)
        if back:
            value = pltpu.roll(value, back, 1)
        return jnp.where(lane == cz - 1, value, 0.0)

    for ref in basis:
        for x in range(HALO):
            for at in (x, tall - 1 - x):
                ref[PAD + at * wide : PAD + (at + 1) * wide, :] = jnp.zeros((wide, cz), F32)
        ref[0:PAD, :] = jnp.zeros((PAD, cz), F32)
        ref[PAD + tall * wide : 2 * PAD + tall * wide, :] = jnp.zeros((PAD, cz), F32)

    def first(x, carry):
        given = spread[pl.ds(pl.multiple_of(x * cy, 8), cy), :]
        extra = jnp.concatenate(
            [top(given[cy - 8 : cy], 1)[8 - HALO : 8], top(given, 0), top(given[0:8], 2)[0:HALO]], axis=0
        )
        at = pl.ds(row(x), wide)
        basis[0][at, :] = (misfit[at, :] + extra) * inverse[at, :]
        return carry

    lax.fori_loop(1, tall - 1, first, 0)
    for k in range(1, ITERS + 1):

        def step(x, carry):
            at = row(x)
            _, total = neighbours(basis[k - 1], at, wide)
            basis[k][pl.ds(at, wide), :] = total * inverse[pl.ds(at, wide), :]
            return carry

        lax.fori_loop(1 + k, tall - 1 - k, step, 0)

    def gather(x, totals):
        at = pl.ds(PAD + (x + HALO) * wide + HALO, cy)
        parts = [ref[at, :] for ref in basis]
        scaled = [(6.0 + inertia[x]) * part for part in parts[:ITERS]]
        out = []
        for m in range(MOMENTS):
            product = scaled[m // 2] * parts[m - m // 2]
            out.append(totals[m] + jnp.sum(product.reshape(cy // 8, 8, cz), axis=0))
        return tuple(out)

    totals = lax.fori_loop(0, cx, gather, tuple(jnp.zeros((8, cz), F32) for _ in range(MOMENTS)))
    lane = lax.broadcasted_iota(jnp.int32, (1, cz), 1)
    line = jnp.zeros((1, cz), F32)
    for m in range(MOMENTS):
        line = jnp.where(lane == m, jnp.sum(totals[m]), line)
    sums[...] = jnp.broadcast_to(line, sums.shape)


def make_basis(misfit, inverse, inertia, own, left, right, devices):
    cx, cy, cz = inertia.shape
    shape = jax.ShapeDtypeStruct(misfit.shape, F32)
    outs = (shape,) * (ITERS + 1) + (jax.ShapeDtypeStruct((devices, cz), F32),)
    return pl.pallas_call(
        functools.partial(basis_kernel, cx, cy, devices),
        out_shape=outs,
        in_specs=[VMEM] * 6,
        out_specs=(VMEM,) * len(outs),
        scratch_shapes=[pltpu.VMEM((own.shape[1], cz), F32)],
        compiler_params=params(),
        cost_estimate=cost(10**7),
        name="basis",
    )(misfit, inverse, inertia, own, left, right)


def finish_kernel(field, inertia, sums, *refs):
    basis, (state, misfit) = refs[: ITERS + 1], refs[ITERS + 1 :]
    cx, cy, cz = field.shape
    wide = cy + 2 * HALO
    line = jnp.sum(sums[...], axis=0, keepdims=True)
    lane = lax.broadcasted_iota(jnp.int32, line.shape, 1)
    moment = [jnp.sum(jnp.where(lane == m, line, 0.0), axis=1, keepdims=True) for m in range(MOMENTS)]

    def product(a, b):
        total = None
        for m in range(len(a) + len(b) - 1):
            weight = None
            for i in range(len(a)):
                if 0 <= m - i < len(b):
                    term = a[i] * b[m - i]
                    weight = term if weight is None else weight + term
            term = weight * moment[m]
            total = term if total is None else total + term
        return total

    one = jnp.ones((1, 1), F32)
    zero = jnp.zeros((1, 1), F32)
    precond, course, guess = [one], [one], [zero] * ITERS
    norm = moment[0]
    for iteration in range(ITERS):
        image = [a - b for a, b in zip(course + [zero], [zero] + course)]
        multiplier = norm / product(course, image)
        guess = [g + multiplier * c for g, c in zip(guess, course + [zero] * ITERS)]
        precond = [a - multiplier * b for a, b in zip(precond + [zero] * 2, image)]
        if iteration + 1 < ITERS:
            following = product(precond, precond)
            ratio = following / norm
            course = [a + ratio * b for a, b in zip(precond, course + [zero])]
            norm = following
    guess = [jnp.broadcast_to(g, (1, cz)) for g in guess]
    precond = [jnp.broadcast_to(g, (1, cz)) for g in precond]

    def step(x, carry):
        at = pl.ds(PAD + (x + HALO) * wide + HALO, cy)
        parts = [ref[at, :] for ref in basis]
        value = field[x]
        for g, part in zip(guess, parts):
            value = value + g * part
        state[x] = value
        rest = precond[0] * parts[0]
        for g, part in zip(precond[1:], parts[1:]):
            rest = rest + g * part
        misfit[x] = (6.0 + inertia[x]) * rest
        return carry

    lax.fori_loop(0, cx, step, 0)


def finish(field, inertia, sums, basis):
    shape = jax.ShapeDtypeStruct(field.shape, F32)
    return pl.pallas_call(
        finish_kernel,
        out_shape=(shape, shape),
        in_specs=[VMEM] * (3 + len(basis)),
        out_specs=(VMEM, VMEM),
        compiler_params=params(),
        cost_estimate=cost(10**6),
        name="finish",
    )(field, inertia, sums, *basis)


def per_device(field, inertia, current, factors, holder, slot):
    count = lax.axis_size("fluid")
    devices = count * lax.axis_size("solid")
    cy = field.shape[1]
    holder = holder.reshape(1, -1)
    slot = slot.reshape(1, -1)

    def swap(value, k):
        return lax.ppermute(value, "fluid", [(i, i ^ k) for i in range(count)])

    blocks = {0: current}
    for k in range(count - 2, 0, -2):
        blocks[k] = swap(current, k)
    head, tail = edges(field, inertia, factors, slot, holder)
    below = lax.ppermute(tail, "fluid", shift("fluid", 1))
    above = lax.ppermute(head, "fluid", shift("fluid", -1))
    for k in range(0, count, 2):
        blocks[k + 1] = swap(blocks[k], 1)
    first, last = sides(field, inertia, below, above)
    left = lax.ppermute(last, "solid", shift("solid", 1))
    right = lax.ppermute(first, "solid", shift("solid", -1))
    own = sources([blocks[k] for k in range(count)], factors, slot, holder, below, above, cy)
    own_left = lax.ppermute(own, "solid", shift("solid", 1))
    own_right = lax.ppermute(own, "solid", shift("solid", -1))
    misfit, inverse = widen(field, inertia, below, above, left, right)
    *basis, sums = make_basis(misfit, inverse, inertia, own, own_left, own_right, devices)
    sums = lax.all_to_all(sums, BOTH, 0, 0, tiled=True)
    return finish(field, inertia, sums, basis)


def solution(mesh):
    return jax.shard_map(
        per_device,
        mesh=mesh,
        in_specs=(
            P("fluid", "solid", None),
            P("fluid", "solid", None),
            P(None, ("fluid", "solid")),
            P(None, ("fluid", "solid")),
            P(("fluid", "solid"), None),
            P(("fluid", "solid")),
        ),
        out_specs=(P("fluid", "solid", None), P("fluid", "solid", None)),
        check_vma=False,
    )
```

time: 250 us -> 62.6 us (0.25)
  blocking collectives: 124 us -> 12.4 us
  waiting for transfers between devices: 40.2 us -> 1.84 us
  between operations: 24 us -> 0.82 us
  Pallas kernels: 0 us -> 19.1 us
  other arithmetic: 18.4 us -> 0 us
  starting transfers between devices: 31.2 us -> 23.5 us
  local copies, waits for them, and re-layouts: 10.6 us -> 4.43 us
    psum x3 -> x0, blocking collectives: 124 us -> none  [paired_sums(): lax.psum((jnp.sum(equation_misfit * precond), jnp.sum(image * precond)),...]
    ppermute x16 -> x13, waiting for transfers between devices: 28.4 us -> 1.84 us  [the longest x7 1.82 us: swap(): return lax.ppermute(value, 'fluid', [(i, i ^ k) for i in range(count)])]
    pallas_call x0 -> x6, Pallas kernels: none -> 19.1 us  [the longest x1 12.3 us: make_basis(): pl.pallas_call(functools.partial(basis_kernel, cx, cy, devices), out_shap...]
    all_to_all x0 -> x1, blocking collectives: none -> 12.4 us  [per_device(): sums = lax.all_to_all(sums, BOTH, 0, 0, tiled=True)]
    all_gather x1 -> x0, waiting for transfers between devices: 11.8 us -> none  [per_device(): lax.all_gather(boundary_energy_current, 'fluid', axis=1, tiled=True)]
    ppermute x16 -> x13, starting transfers between devices: 31.1 us -> 23.5 us  [the longest x7 8.75 us: swap(): return lax.ppermute(value, 'fluid', [(i, i ^ k) for i in range(count)])]
    reduce_sum x4 -> x0, other arithmetic: 5.35 us -> none  [the longest x3 4.98 us: paired_sums(): jnp.sum(image * precond)]
    gather x1 -> x0, local copies, waits for them, and re-layouts: 4.39 us -> none  [per_device(): picked = jnp.take(gathered, columns, axis=1)]
  transfers between devices with their start and end apart: 17 -> 13, of which waited for: 11 -> 4; matrix products, arithmetic and copies ran while one was open for 2% -> 0% of each run, Pallas kernels for 0% -> 8%
where the time goes in v1:
time: 62.6 us; the launch traced here: 62.1 us
  starting transfers between devices  23.5 us (38%)
  Pallas kernels  19.1 us (31%)
  blocking collectives  12.4 us (20%)
  local copies, waits for them, and re-layouts  4.43 us (7%)
  waiting for transfers between devices  1.84 us (3%)
  between operations  0.82 us (1%)
    all_to_all x1, blocking collectives, per_device(): sums = lax.all_to_all(sums, BOTH, 0, 0, tiled=True)  12.4 us
    pallas_call x1, Pallas kernels, make_basis(): pl.pallas_call(functools.partial(basis_kernel, cx, cy, devices), out_shap...  12.3 us
    ppermute x7, starting transfers between devices, swap(): return lax.ppermute(value, 'fluid', [(i, i ^ k) for i in range(count)])  8.75 us
    ppermute x1, starting transfers between devices, per_device(): own_left = lax.ppermute(own, 'solid', shift('solid', 1))  4.55 us
    unnamed x22, local copies, waits for them, and re-layouts  4.43 us
    pallas_call x1, Pallas kernels, widen(): pl.pallas_call(widen_kernel, out_shape=(shape, shape), in_specs=[VMEM] *...  3.59 us
    ppermute x1, starting transfers between devices, per_device(): left = lax.ppermute(last, 'solid', shift('solid', 1))  3.49 us
    ppermute x1, starting transfers between devices, per_device(): below = lax.ppermute(tail, 'fluid', shift('fluid', 1))  2.54 us
  transfers between devices with their start and end apart: 13, of which 4 were waited for; matrix products, arithmetic and copies ran while one was open for 0% of the time, Pallas kernels for 8%

profile of v1, /device:TPU:0, one launch (start us, length us, event | category | flops | bytes accessed | tf_op | source)
XLA Modules:
  0.0 62.1 jit_solution(2016383605169847430)
XLA Ops:
  0.6 0.0 copy-start
  0.6 1.0 %copy-done = f32[32,32,128]{2,1,0:T(8,128)S(1)} copy-done((f32[32,32,128]{2,1,0:T(8,128)S(1)}, f32[32,32,128]{2,1,0:T(8,128)}, u32[]{:S(2)}) %copy-start) | copy-done | bytes 524312
  1.7 0.0 copy-start.2
  1.7 1.0 %copy-done.2 = f32[32,32,128]{2,1,0:T(8,128)S(1)} copy-done((f32[32,32,128]{2,1,0:T(8,128)S(1)}, f32[32,32,128]{2,1,0:T(8,128)}, u32[]{:S(2)}) %copy-start.2) | copy-done | bytes 524312
  2.7 0.0 copy-start.4
  2.7 0.9 %copy-done.4 = f32[64,1024]{1,0:T(8,128)S(1)} copy-done((f32[64,1024]{1,0:T(8,128)S(1)}, f32[64,1024]{1,0:T(8,128)}, u32[]{:S(2)}) %copy-start.4) | copy-done | bytes 262168
  3.7 0.0 copy-start.7
  3.7 0.7 %copy-done.7 = s32[1024]{0:T(1024)S(1)} copy-done((s32[1024]{0:T(1024)S(1)}, s32[1024]{0:T(1024)}, u32[]{:S(2)}) %copy-start.7) | copy-done | bytes 4120
  4.4 0.0 copy-start.9
  4.4 0.7 %copy-done.9 = s32[1024,1]{0,1:T(1,128)S(1)} copy-done((s32[1024,1]{0,1:T(1,128)S(1)}, s32[1024,1]{0,1:T(1,128)}, u32[]{:S(2)}) %copy-start.9) | copy-done | bytes 4120
  5.0 0.0 copy-start.6
  5.1 2.5 %collective-permute-start = (f32[296,128]{1,0:T(8,128)S(1)}, f32[296,128]{1,0:T(8,128)S(1)}, u32[]{:S(2)}, u32[]{:S(2)}) collective-permute-start(f32[296,128]{1,0:T(8,128)S(1)} %get-tuple-element.13), channel_id=1, source_target_pairs={{0,4},{4,8},{8,12},{12,16},{16,20},{20,24},{24,28},{1,5},{5,9},{9,... | collective-permute-start | bytes 454664 | tf_op jit(solution)/shard_map/ppermute | solution.py:419
  7.6 0.0 copy-start.5
  7.6 1.4 %collective-permute-start.1 = (f32[296,128]{1,0:T(8,128)S(1)}, f32[296,128]{1,0:T(8,128)S(1)}, u32[]{:S(2)}, u32[]{:S(2)}) collective-permute-start(f32[296,128]{1,0:T(8,128)S(1)} %get-tuple-element.14), channel_id=1, source_target_pairs={{4,0},{8,4},{12,8},{16,12},{20,16},{24,20},{28,24},{5,1},{9,5},{13... | collective-permute-start | bytes 454664 | tf_op jit(solution)/shard_map/ppermute | solution.py:420
  9.1 0.0 copy-done.6
  9.1 5.8 %collective-permute-start.7 = (f32[64,512]{1,0:T(8,128)S(1)}, f32[64,512]{1,0:T(8,128)S(1)}, u32[]{:S(2)}, u32[]{:S(2)}) collective-permute-start(f32[64,512]{1,0:T(8,128)S(1)} %copy-done.6), channel_id=1, source_target_pairs={{0,16},{4,20},{8,24},{12,28},{16,0},{20,4},{24,8},{28,12},{1,17},{... | collective-permute-start | bytes 393224 | tf_op jit(solution)/shard_map/ppermute | solution.py:413
  14.9 0.6 collective-permute-start.5
  15.5 0.0 collective-permute-start.4
  15.5 0.0 collective-permute-done.below.refs_11_
  15.5 0.9 %collective-permute-start.9 = (f32[64,512]{1,0:T(8,128)S(1)}, f32[64,512]{1,0:T(8,128)S(1)}, u32[]{:S(2)}, u32[]{:S(2)}) collective-permute-start(f32[64,512]{1,0:T(8,128)S(1)} %copy-done.6), channel_id=1, source_target_pairs={{0,24},{4,28},{8,16},{12,20},{16,8},{20,12},{24,0},{28,4},{1,25},{... | collective-permute-start | bytes 393224 | tf_op jit(solution)/shard_map/ppermute | solution.py:413
  16.4 0.0 collective-permute-done.1.above.refs_12_
  16.4 0.0 copy-start.8
  16.4 0.0 copy-start.10
  16.4 0.1 sides.1
  16.5 3.5 %collective-permute-start.2 = (f32[40,8,128]{2,1,0:T(8,128)S(1)}, f32[40,8,128]{2,1,0:T(8,128)S(1)}, u32[]{:S(2)}, u32[]{:S(2)}) collective-permute-start(f32[40,8,128]{2,1,0:T(8,128)S(1)} %get-tuple-element.15), channel_id=1, source_target_pairs={{0,1},{1,2},{2,3},{4,5},{5,6},{6,7},{8,9},{9,10},{10,11},{12,13},{... | collective-permute-start | bytes 491528 | tf_op jit(solution)/shard_map/ppermute | solution.py:424
  20.0 0.0 collective-permute-done.7.refs_4_
  20.0 0.0 copy-start.1
  20.1 0.0 copy-start.3
  20.1 1.4 %collective-permute-start.3 = (f32[40,8,128]{2,1,0:T(8,128)S(1)}, f32[40,8,128]{2,1,0:T(8,128)S(1)}, u32[]{:S(2)}, u32[]{:S(2)}) collective-permute-start(f32[40,8,128]{2,1,0:T(8,128)S(1)} %get-tuple-element.16), channel_id=1, source_target_pairs={{1,0},{2,1},{3,2},{5,4},{6,5},{7,6},{9,8},{10,9},{11,10},{13,12},{... | collective-permute-start | bytes 491528 | tf_op jit(solution)/shard_map/ppermute | solution.py:425
  21.5 0.0 collective-permute-done.5.refs_2_
  21.5 1.3 %collective-permute-start.8 = (f32[64,512]{1,0:T(8,128)S(1)}, f32[64,512]{1,0:T(8,128)S(1)}, u32[]{:S(2)}, u32[]{:S(2)}) collective-permute-start(f32[64,512]{1,0:T(8,128)S(1)} %collective-permute-done.7.refs_4_), channel_id=1, source_target_pairs={{0,4},{4,0},{8,12},{12,8},{16,20},{20,16},{24,28},{28,24},{1,5},{5... | collective-permute-start | bytes 393224 | tf_op jit(solution)/shard_map/ppermute | solution.py:413
  22.8 0.0 collective-permute-done.4.refs_1_
  22.8 0.1 collective-permute-start.6
  22.9 0.5 collective-permute-done.9.refs_6_
  23.4 0.0 collective-permute-start.10
  23.4 0.4 collective-permute-done.8.refs_5_
  23.8 0.4 collective-permute-done.6.refs_3_
  24.2 0.6 collective-permute-done.10.refs_7_
  24.7 0.0 copy-done.5
  24.7 0.0 copy-done.8
  24.7 0.0 copy-done.10
  24.7 1.6 %sources.1.own = f32[1,1280]{1,0:T(1,128)S(1)} custom-call(f32[64,512]{1,0:T(8,128)S(1)} %copy-done.6, f32[64,512]{1,0:T(8,128)S(1)} %collective-permute-done.4.refs_1_, f32[64,512]{1,0:T(8,128)S(1)} %collective-permute-done.5.refs_2_, f32[64,512]{1,0:T(8,128)S(1)} %collective-permute-done.6.refs_3_, f32[64,512]{1,0:T(8,128)S(1)} %collective-permute-done.7.refs_4_, ...), custom_call_target="tpu_custom_call" | custom-call | flops 100000000 | tf_op jit(solution)/shard_map/sources/pallas_call | solution.py:152
  26.3 1.3 %collective-permute-start.12 = (f32[1,1280]{1,0:T(1,128)S(1)}, f32[1,1280]{1,0:T(1,128)S(1)}, u32[]{:S(2)}, u32[]{:S(2)}) collective-permute-start(f32[1,1280]{1,0:T(1,128)S(1)} %sources.1.own), channel_id=1, source_target_pairs={{1,0},{2,1},{3,2},{5,4},{6,5},{7,6},{9,8},{10,9},{11,10},{13,12},{... | collective-permute-start | bytes 15368 | tf_op jit(solution)/shard_map/ppermute | solution.py:428
  27.6 4.5 %collective-permute-start.11 = (f32[1,1280]{1,0:T(1,128)S(1)}, f32[1,1280]{1,0:T(1,128)S(1)}, u32[]{:S(2)}, u32[]{:S(2)}) collective-permute-start(f32[1,1280]{1,0:T(1,128)S(1)} %sources.1.own), channel_id=1, source_target_pairs={{0,1},{1,2},{2,3},{4,5},{5,6},{6,7},{8,9},{9,10},{10,11},{12,13},{... | collective-permute-start | bytes 15368 | tf_op jit(solution)/shard_map/ppermute | solution.py:427
  32.1 0.0 collective-permute-done.2.left
  32.2 0.0 collective-permute-done.3.right
  32.2 0.0 copy-done.1
  32.2 0.0 copy-done.3
  32.2 3.6 %widen.1 = (f32[1616,128]{1,0:T(8,128)S(1)}, f32[1616,128]{1,0:T(8,128)S(1)}) custom-call(f32[32,32,128]{2,1,0:T(8,128)S(1)} %copy-done.3, f32[32,32,128]{2,1,0:T(8,128)S(1)} %copy-done.1, f32[296,128]{1,0:T(8,128)S(1)} %collective-permute-done.below.refs_11_, f32[296,128]{1,0:T(8,128)S(1)} %collective-permute-done.1.above.refs_12_, ...), custom_call_target="tpu_custom_call" | custom-call | flops 10000000 | tf_op jit(solution)/shard_map/widen/pallas_call | solution.py:238
  35.8 0.0 collective-permute-done.12.right
  35.8 0.0 collective-permute-done.11.left
  35.8 12.3 %basis.1 = (f32[1616,128]{1,0:T(8,128)S(1)}, f32[1616,128]{1,0:T(8,128)S(1)}, f32[1616,128]{1,0:T(8,128)S(1)}, f32[1616,128]{1,0:T(8,128)S(1)}, f32[32,128]{1,0:T(8,128)S(1)}) custom-call(f32[1616,128]{1,0:T(8,128)S(1)} %get-tuple-element.17.misfit, f32[1616,128]{1,0:T(8,128)S(1)} %get-tuple-element.18.inverse, f32[32,32,128]{2,1,0:T(8,128)S(1)} %copy-done.1, ...), custom_call_target="tpu_custom_call" | custom-call | flops 10000000 | tf_op jit(solution)/shard_map/basis/pallas_call | solution.py:327
  48.1 12.4 %all_to_all.11 = f32[32,1,128]{2,1,0:T(1,128)S(1)} all-to-all(f32[32,1,128]{2,1,0:T(1,128)S(1)} %bitcast.11), channel_id=1, replica_groups=mesh['fluid'=8,'solid'=4] {'fluid','solid'}, dimensions={0} | all-to-all | bytes 32768 | tf_op jit(solution)/shard_map/all_to_all | solution.py:431
  60.6 1.5 %finish.1 = (f32[32,32,128]{2,1,0:T(8,128)}, f32[32,32,128]{2,1,0:T(8,128)}) custom-call(f32[32,32,128]{2,1,0:T(8,128)S(1)} %copy-done.3, f32[32,32,128]{2,1,0:T(8,128)S(1)} %copy-done.1, f32[32,128]{1,0:T(8,128)S(1)} %bitcast.6, f32[1616,128]{1,0:T(8,128)S(1)} %get-tuple-element.20.refs_0_, f32[1616,128]{1,0:T(8,128)S(1)} %get-tuple-element.21.refs_1_, ...), custom_call_target="tpu_custom_call" | custom-call | flops 1000000 | tf_op jit(solution)/shard_map/finish/pallas_call | solution.py:394
  (1 shorter events, 0.0 us)
Async XLA Ops:
  0.6 1.0 %copy-start = (f32[32,32,128]{2,1,0:T(8,128)S(1)}, f32[32,32,128]{2,1,0:T(8,128)}, u32[]{:S(2)}) copy-start(f32[32,32,128]{2,1,0:T(8,128)} %inertia.9) | copy-start | bytes 1572868
  1.7 1.0 %copy-start.2 = (f32[32,32,128]{2,1,0:T(8,128)S(1)}, f32[32,32,128]{2,1,0:T(8,128)}, u32[]{:S(2)}) copy-start(f32[32,32,128]{2,1,0:T(8,128)} %field.7) | copy-start | bytes 1572868
  2.7 0.9 %copy-start.4 = (f32[64,1024]{1,0:T(8,128)S(1)}, f32[64,1024]{1,0:T(8,128)}, u32[]{:S(2)}) copy-start(f32[64,1024]{1,0:T(8,128)} %refs_8_.1) | copy-start | bytes 786436
  3.7 0.7 %copy-start.7 = (s32[1024]{0:T(1024)S(1)}, s32[1024]{0:T(1024)}, u32[]{:S(2)}) copy-start(s32[1024]{0:T(1024)} %param.11) | copy-start | bytes 12292
  4.4 0.7 %copy-start.9 = (s32[1024,1]{0,1:T(1,128)S(1)}, s32[1024,1]{0,1:T(1,128)}, u32[]{:S(2)}) copy-start(s32[1024,1]{0,1:T(1,128)} %param.10) | copy-start | bytes 12292
  5.0 4.0 %copy-start.6 = (f32[64,512]{1,0:T(8,128)S(1)}, f32[64,512]{1,0:T(8,128)}, u32[]{:S(2)}) copy-start(f32[64,512]{1,0:T(8,128)} %refs_0_.1) | copy-start | bytes 393220
  5.1 10.4 %collective-permute-start = (f32[296,128]{1,0:T(8,128)S(1)}, f32[296,128]{1,0:T(8,128)S(1)}, u32[]{:S(2)}, u32[]{:S(2)}) collective-permute-start(f32[296,128]{1,0:T(8,128)S(1)} %get-tuple-element.13), channel_id=1, source_target_pairs={{0,4},{4,8},{8,12},{12,16},{16,20},{20,24},{24,28},{1,5},{5,9},{9,... | collective-permute-start | bytes 454664 | tf_op jit(solution)/shard_map/ppermute | solution.py:419
  7.6 17.1 %copy-start.5 = (f32[64,1024]{1,0:T(8,128)S(1)}, f32[64,1024]{1,0:T(8,128)}, u32[]{:S(2)}) copy-start(f32[64,1024]{1,0:T(8,128)} %refs_8_.1) | copy-start | bytes 786436
  7.6 8.8 %collective-permute-start.1 = (f32[296,128]{1,0:T(8,128)S(1)}, f32[296,128]{1,0:T(8,128)S(1)}, u32[]{:S(2)}, u32[]{:S(2)}) collective-permute-start(f32[296,128]{1,0:T(8,128)S(1)} %get-tuple-element.14), channel_id=1, source_target_pairs={{4,0},{8,4},{12,8},{16,12},{20,16},{24,20},{28,24},{5,1},{9,5},{13... | collective-permute-start | bytes 454664 | tf_op jit(solution)/shard_map/ppermute | solution.py:420
  9.1 11.0 %collective-permute-start.7 = (f32[64,512]{1,0:T(8,128)S(1)}, f32[64,512]{1,0:T(8,128)S(1)}, u32[]{:S(2)}, u32[]{:S(2)}) collective-permute-start(f32[64,512]{1,0:T(8,128)S(1)} %copy-done.6), channel_id=1, source_target_pairs={{0,16},{4,20},{8,24},{12,28},{16,0},{20,4},{24,8},{28,12},{1,17},{... | collective-permute-start | bytes 393224 | tf_op jit(solution)/shard_map/ppermute | solution.py:413
  14.9 6.6 %collective-permute-start.5 = (f32[64,512]{1,0:T(8,128)S(1)}, f32[64,512]{1,0:T(8,128)S(1)}, u32[]{:S(2)}, u32[]{:S(2)}) collective-permute-start(f32[64,512]{1,0:T(8,128)S(1)} %copy-done.6), channel_id=1, source_target_pairs={{0,8},{4,12},{8,0},{12,4},{16,24},{20,28},{24,16},{28,20},{1,9},{5... | collective-permute-start | bytes 393224 | tf_op jit(solution)/shard_map/ppermute | solution.py:413
  15.5 7.3 %collective-permute-start.4 = (f32[64,512]{1,0:T(8,128)S(1)}, f32[64,512]{1,0:T(8,128)S(1)}, u32[]{:S(2)}, u32[]{:S(2)}) collective-permute-start(f32[64,512]{1,0:T(8,128)S(1)} %copy-done.6), channel_id=1, source_target_pairs={{0,4},{4,0},{8,12},{12,8},{16,20},{20,16},{24,28},{28,24},{1,5},{5... | collective-permute-start | bytes 393224 | tf_op jit(solution)/shard_map/ppermute | solution.py:413
  15.5 7.9 %collective-permute-start.9 = (f32[64,512]{1,0:T(8,128)S(1)}, f32[64,512]{1,0:T(8,128)S(1)}, u32[]{:S(2)}, u32[]{:S(2)}) collective-permute-start(f32[64,512]{1,0:T(8,128)S(1)} %copy-done.6), channel_id=1, source_target_pairs={{0,24},{4,28},{8,16},{12,20},{16,8},{20,12},{24,0},{28,4},{1,25},{... | collective-permute-start | bytes 393224 | tf_op jit(solution)/shard_map/ppermute | solution.py:413
  16.4 8.3 %copy-start.8 = (s32[1024]{0:T(1024)S(1)}, s32[1024]{0:T(1024)}, u32[]{:S(2)}) copy-start(s32[1024]{0:T(1024)} %param.11) | copy-start | bytes 12292
  16.4 8.3 %copy-start.10 = (s32[1024,1]{0,1:T(1,128)S(1)}, s32[1024,1]{0,1:T(1,128)}, u32[]{:S(2)}) copy-start(s32[1024,1]{0,1:T(1,128)} %param.10) | copy-start | bytes 12292
  16.5 15.6 %collective-permute-start.2 = (f32[40,8,128]{2,1,0:T(8,128)S(1)}, f32[40,8,128]{2,1,0:T(8,128)S(1)}, u32[]{:S(2)}, u32[]{:S(2)}) collective-permute-start(f32[40,8,128]{2,1,0:T(8,128)S(1)} %get-tuple-element.15), channel_id=1, source_target_pairs={{0,1},{1,2},{2,3},{4,5},{5,6},{6,7},{8,9},{9,10},{10,11},{12,13},{... | collective-permute-start | bytes 491528 | tf_op jit(solution)/shard_map/ppermute | solution.py:424
  20.0 12.1 %copy-start.1 = (f32[32,32,128]{2,1,0:T(8,128)S(1)}, f32[32,32,128]{2,1,0:T(8,128)}, u32[]{:S(2)}) copy-start(f32[32,32,128]{2,1,0:T(8,128)} %inertia.9) | copy-start | bytes 1572868
  20.1 12.1 %copy-start.3 = (f32[32,32,128]{2,1,0:T(8,128)S(1)}, f32[32,32,128]{2,1,0:T(8,128)}, u32[]{:S(2)}) copy-start(f32[32,32,128]{2,1,0:T(8,128)} %field.7) | copy-start | bytes 1572868
  20.1 12.1 %collective-permute-start.3 = (f32[40,8,128]{2,1,0:T(8,128)S(1)}, f32[40,8,128]{2,1,0:T(8,128)S(1)}, u32[]{:S(2)}, u32[]{:S(2)}) collective-permute-start(f32[40,8,128]{2,1,0:T(8,128)S(1)} %get-tuple-element.16), channel_id=1, source_target_pairs={{1,0},{2,1},{3,2},{5,4},{6,5},{7,6},{9,8},{10,9},{11,10},{13,12},{... | collective-permute-start | bytes 491528 | tf_op jit(solution)/shard_map/ppermute | solution.py:425
  21.5 2.3 %collective-permute-start.8 = (f32[64,512]{1,0:T(8,128)S(1)}, f32[64,512]{1,0:T(8,128)S(1)}, u32[]{:S(2)}, u32[]{:S(2)}) collective-permute-start(f32[64,512]{1,0:T(8,128)S(1)} %collective-permute-done.7.refs_4_), channel_id=1, source_target_pairs={{0,4},{4,0},{8,12},{12,8},{16,20},{20,16},{24,28},{28,24},{1,5},{5... | collective-permute-start | bytes 393224 | tf_op jit(solution)/shard_map/ppermute | solution.py:413
  22.8 1.3 %collective-permute-start.6 = (f32[64,512]{1,0:T(8,128)S(1)}, f32[64,512]{1,0:T(8,128)S(1)}, u32[]{:S(2)}, u32[]{:S(2)}) collective-permute-start(f32[64,512]{1,0:T(8,128)S(1)} %collective-permute-done.5.refs_2_), channel_id=1, source_target_pairs={{0,4},{4,0},{8,12},{12,8},{16,20},{20,16},{24,28},{28,24},{1,5},{5... | collective-permute-start | bytes 393224 | tf_op jit(solution)/shard_map/ppermute | solution.py:413
  23.4 1.3 %collective-permute-start.10 = (f32[64,512]{1,0:T(8,128)S(1)}, f32[64,512]{1,0:T(8,128)S(1)}, u32[]{:S(2)}, u32[]{:S(2)}) collective-permute-start(f32[64,512]{1,0:T(8,128)S(1)} %collective-permute-done.9.refs_6_), channel_id=1, source_target_pairs={{0,4},{4,0},{8,12},{12,8},{16,20},{20,16},{24,28},{28,24},{1,5},{5... | collective-permute-start | bytes 393224 | tf_op jit(solution)/shard_map/ppermute | solution.py:413
  26.3 9.5 %collective-permute-start.12 = (f32[1,1280]{1,0:T(1,128)S(1)}, f32[1,1280]{1,0:T(1,128)S(1)}, u32[]{:S(2)}, u32[]{:S(2)}) collective-permute-start(f32[1,1280]{1,0:T(1,128)S(1)} %sources.1.own), channel_id=1, source_target_pairs={{1,0},{2,1},{3,2},{5,4},{6,5},{7,6},{9,8},{10,9},{11,10},{13,12},{... | collective-permute-start | bytes 15368 | tf_op jit(solution)/shard_map/ppermute | solution.py:428
  27.6 8.2 %collective-permute-start.11 = (f32[1,1280]{1,0:T(1,128)S(1)}, f32[1,1280]{1,0:T(1,128)S(1)}, u32[]{:S(2)}, u32[]{:S(2)}) collective-permute-start(f32[1,1280]{1,0:T(1,128)S(1)} %sources.1.own), channel_id=1, source_target_pairs={{0,1},{1,2},{2,3},{4,5},{5,6},{6,7},{8,9},{9,10},{10,11},{12,13},{... | collective-permute-start | bytes 15368 | tf_op jit(solution)/shard_map/ppermute | solution.py:427

commit v2 on v1

v2 whole, which is shorter than its diff:
```python
import functools

import jax
import jax.numpy as jnp
from jax import lax
from jax.experimental import pallas as pl
from jax.experimental.pallas import tpu as pltpu
from jax.sharding import PartitionSpec as P

ITERS = 3
HALO = ITERS + 1
MOMENTS = 2 * ITERS
PAD = 8
BOTH = ("fluid", "solid")
VMEM = pl.BlockSpec(memory_space=pltpu.VMEM)
F32 = jnp.float32
BF16 = jnp.bfloat16


def params():
    return pltpu.CompilerParams(vmem_limit_bytes=24 * 1024 * 1024)


def cost(flops, size=0):
    return pl.CostEstimate(flops=flops, bytes_accessed=size, transcendentals=0)


def shift(axis, step):
    size = lax.axis_size(axis)
    if step > 0:
        return [(i, i + 1) for i in range(size - 1)]
    return [(i + 1, i) for i in range(size - 1)]


def even():
    return lax.rem(lax.axis_index("fluid"), 2) == 0


def edge_kernel(cy, field, inertia, factors, slot, holder, near, far, marks, sems):
    edge = HALO * cy
    thick = (HALO - 1) * cy
    quads, rows = factors.shape
    cells = field.shape[0]
    top = edge + thick
    is_even = even()
    copies = []
    for i, out in enumerate((near, far)):
        at_end = is_even if i == 0 else jnp.logical_not(is_even)
        row = pl.multiple_of(jnp.where(at_end, rows - edge, 0), 128)
        cell = pl.multiple_of(jnp.where(at_end, cells - thick, 0), 8)
        pieces = (
            (field.at[pl.ds(row, edge), :], out.at[0:edge, :]),
            (inertia.at[pl.ds(cell, thick), :], out.at[edge:top, :]),
            (factors.at[:, pl.ds(row, edge)], out.at[top : top + quads, :]),
            (slot.at[:, pl.ds(row, edge)], marks.at[2 * i]),
            (holder.at[:, pl.ds(row, edge)], marks.at[2 * i + 1]),
        )
        for j, (source, target) in enumerate(pieces):
            copies.append(pltpu.make_async_copy(source, target, sems.at[i, j]))
    for copy in copies:
        copy.start()
    for copy in copies:
        copy.wait()
    for i, out in enumerate((near, far)):
        rest = jnp.zeros((6, edge), F32)
        packed = [marks[2 * i].astype(F32), marks[2 * i + 1].astype(F32), rest]
        out[top + quads : top + quads + 8, :] = jnp.concatenate(packed, axis=0)


def edges(field, inertia, factors, slot, holder):
    cx, cy, cz = field.shape
    edge = HALO * cy
    length = edge + (HALO - 1) * cy + factors.shape[0] + 8
    shape = jax.ShapeDtypeStruct((length, cz), F32)
    return pl.pallas_call(
        functools.partial(edge_kernel, cy),
        out_shape=(shape, shape),
        in_specs=[pl.BlockSpec(memory_space=pltpu.HBM)] * 5,
        out_specs=(VMEM, VMEM),
        scratch_shapes=[pltpu.VMEM((4, 1, edge), jnp.int32), pltpu.SemaphoreType.DMA((2, 5))],
        compiler_params=params(),
        cost_estimate=cost(10**5),
        name="edges",
    )(field.reshape(cx * cy, cz), inertia.reshape(cx * cy, cz), factors, slot, holder)


def side_kernel(field, inertia, near, far, first, last):
    cx, cy, cz = field.shape
    edge = HALO * cy
    thin = HALO - 1
    thick = thin * cy
    tall = cx + 2 * HALO
    is_even = even()
    got = (
        jnp.where(is_even, far[0 : edge + thick, :], near[0 : edge + thick, :]),
        jnp.where(is_even, near[0 : edge + thick, :], far[0 : edge + thick, :]),
    )
    for out, field_at, inertia_at in ((first, 0, 0), (last, cy - HALO, cy - thin)):
        for slabs, at, inertia_to in ((got[0], 0, 1), (got[1], cx + HALO, cx + HALO)):
            slab = slabs[0:edge].reshape(HALO, cy, cz)
            out[at : at + HALO, 0:HALO, :] = slab[:, field_at : field_at + HALO, :]
            slab = slabs[edge : edge + thick].reshape(thin, cy, cz)
            out[inertia_to : inertia_to + thin, HALO : HALO + thin, :] = slab[:, inertia_at : inertia_at + thin, :]
        out[HALO : HALO + cx, 0:HALO, :] = field[:, field_at : field_at + HALO, :]
        out[HALO : HALO + cx, HALO : HALO + thin, :] = inertia[:, inertia_at : inertia_at + thin, :]
        zero = jnp.zeros((1, thin, cz), F32)
        out[0:1, HALO : HALO + thin, :] = zero
        out[tall - 1 : tall, HALO : HALO + thin, :] = zero
        out[:, 2 * HALO - 1 : 2 * HALO, :] = jnp.zeros((tall, 1, cz), F32)


def sides(field, inertia, near, far):
    cx, cy, cz = field.shape
    shape = jax.ShapeDtypeStruct((cx + 2 * HALO, 2 * HALO, cz), F32)
    return pl.pallas_call(
        side_kernel,
        out_shape=(shape, shape),
        in_specs=[VMEM] * 4,
        out_specs=(VMEM, VMEM),
        compiler_params=params(),
        cost_estimate=cost(10**5),
        name="sides",
    )(field, inertia, near, far)


def source_kernel(count, cy, thick, *refs):
    blocks = refs[:count]
    factors, slot, holder, near, far, out, table, picked = refs[count:]
    quads, faces = blocks[0].shape
    rows = factors.shape[1]
    edge = HALO * cy
    top = edge + thick
    me = lax.axis_index("fluid")
    for k in range(count):
        value = blocks[k][...]
        high = value.astype(BF16)
        low = (value - high.astype(F32)).astype(BF16)
        table[2 * k * quads : (2 * k + 1) * quads, :] = high
        table[(2 * k + 1) * quads : (2 * k + 2) * quads, :] = low

    def part(slots, holders, weights, width):
        spot = lax.broadcasted_iota(jnp.int32, (faces, width), 0)
        chosen = jnp.where(spot == slots, 1.0, 0.0).astype(BF16)
        picked[:, 0:width] = jnp.dot(table[...], chosen, preferred_element_type=F32)
        total = jnp.zeros((quads, width), F32)
        for k in range(count):
            high = picked[2 * k * quads : (2 * k + 1) * quads, 0:width]
            low = picked[(2 * k + 1) * quads : (2 * k + 2) * quads, 0:width]
            total = total + jnp.where(holders == (me ^ k), high + low, 0.0)
        return jnp.sum(total * weights, axis=0, keepdims=True)

    is_even = even()

    def side(one, other):
        got = jnp.where(is_even, one[top : top + quads + 8, :], other[top : top + quads + 8, :])
        marks = got[quads : quads + 8].astype(jnp.int32)
        return marks[0:1], marks[1:2], got[0:quads]

    slots, holders, weights = (jnp.concatenate(t, axis=1) for t in zip(side(far, near), side(near, far)))
    both = part(slots, holders, weights, 2 * edge)
    out[:, 0:edge] = both[:, 0:edge]
    out[:, edge + rows : 2 * edge + rows] = both[:, edge : 2 * edge]
    width = 2 * edge
    for at in range(0, rows, width):
        spots = slice(at, at + width)
        out[:, edge + at : edge + at + width] = part(slot[:, spots], holder[:, spots], factors[:, spots], width)


def sources(blocks, factors, slot, holder, near, far, cy):
    count = len(blocks)
    quads, rows = factors.shape
    faces = blocks[0].shape[1]
    edge = HALO * cy
    return pl.pallas_call(
        functools.partial(source_kernel, count, cy, (HALO - 1) * cy),
        out_shape=jax.ShapeDtypeStruct((1, rows + 2 * edge), F32),
        in_specs=[VMEM] * (count + 5),
        out_specs=VMEM,
        scratch_shapes=[
            pltpu.VMEM((2 * quads * count, faces), BF16),
            pltpu.VMEM((2 * quads * count, 2 * edge), F32),
        ],
        compiler_params=params(),
        cost_estimate=cost(10**8),
        name="sources",
    )(*blocks, factors, slot, holder, near, far)


def neighbours(ref, at, wide, before, centre, after):
    lane = lax.broadcasted_iota(jnp.int32, centre.shape, 1)
    depth = centre.shape[1]
    lower = jnp.where(lane == 0, 0.0, pltpu.roll(centre, 1, 1))
    upper = jnp.where(lane == depth - 1, 0.0, pltpu.roll(centre, depth - 1, 1))
    total = before + after
    total = total + (ref[at - 1 : at - 1 + wide, :] + ref[at + 1 : at + 1 + wide, :])
    return total + (lower + upper)


def sweep(ref, wide, low, high, out):
    def plane(x):
        return ref[PAD + x * wide : PAD + (x + 1) * wide, :]

    before, centre = plane(low - 1), plane(low)
    for x in range(low, high):
        after = plane(x + 1)
        out(x, neighbours(ref, PAD + x * wide, wide, before, centre, after), centre)
        before, centre = centre, after


def clear(ref, low, high):
    ref[low:high, :] = jnp.zeros((high - low, ref.shape[1]), F32)


def widen_kernel(field, inertia, near, far, left, right, misfit, inverse, wide_field):
    cx, cy, cz = field.shape
    edge = HALO * cy
    thin = HALO - 1
    wide = cy + 2 * HALO
    tall = cx + 2 * HALO
    is_even = even()
    clear(wide_field, 0, PAD)
    clear(wide_field, PAD + tall * wide, 2 * PAD + tall * wide)
    none = jnp.zeros((1, cz), F32)

    def ends(one, other, low, high):
        return jnp.where(is_even, one[low:high, :], other[low:high, :])

    for x in range(tall):
        if x < HALO:
            middle = ends(far, near, x * cy, (x + 1) * cy)
            at = edge + (x - 1) * cy
            capacity = ends(far, near, at, at + cy) if x > 0 else None
        elif x < cx + HALO:
            middle, capacity = field[x - HALO], inertia[x - HALO]
        else:
            at = (x - cx - HALO) * cy
            middle = ends(near, far, at, at + cy)
            at = edge + at
            capacity = ends(near, far, at, at + cy) if x < tall - 1 else None
        before, after = left[x], right[x]
        here = slice(PAD + x * wide, PAD + (x + 1) * wide)
        wide_field[here, :] = jnp.concatenate([before[0:HALO], middle, after[0:HALO]], axis=0)
        if capacity is not None:
            full = [none, before[HALO : HALO + thin], capacity, after[HALO : HALO + thin], none]
            full = jnp.concatenate(full, axis=0)
            inverse[here, :] = jnp.where(full > 0.0, 1.0 / (6.0 + full), 0.0)

    def put(x, total, centre):
        misfit[PAD + x * wide : PAD + (x + 1) * wide, :] = total - 6.0 * centre

    sweep(wide_field, wide, 1, tall - 1, put)


def widen(field, inertia, near, far, left, right):
    cx, cy, cz = field.shape
    length = (cx + 2 * HALO) * (cy + 2 * HALO) + 2 * PAD
    shape = jax.ShapeDtypeStruct((length, cz), F32)
    return pl.pallas_call(
        widen_kernel,
        out_shape=(shape, shape),
        in_specs=[VMEM] * 6,
        out_specs=(VMEM, VMEM),
        scratch_shapes=[pltpu.VMEM((length, cz), F32)],
        compiler_params=params(),
        cost_estimate=cost(10**7),
        name="widen",
    )(field, inertia, near, far, left, right)


def basis_kernel(cx, cy, devices, misfit, inverse, inertia, own, left, right, *outs):
    basis, sums, spread = outs[: ITERS + 1], outs[ITERS + 1], outs[ITERS + 2]
    cz = misfit.shape[1]
    wide = cy + 2 * HALO
    tall = cx + 2 * HALO

    rows = jnp.concatenate([own[...], left[...], right[...]], axis=0)
    high = rows.astype(BF16)
    rest = rows - high.astype(F32)
    mid = rest.astype(BF16)
    low = (rest - mid.astype(F32)).astype(BF16)
    stack = jnp.concatenate([high.astype(F32), mid.astype(F32), low.astype(F32)], axis=0)
    index = lax.broadcasted_iota(jnp.int32, (9, cz), 0)
    lane9 = lax.broadcasted_iota(jnp.int32, (9, cz), 1)
    place = jnp.where(lane9 == cz - 1 - index % 3, 1.0, 0.0)
    spread[...] = lax.dot_general(
        stack.astype(BF16), place.astype(BF16), (((0,), (0,)), ((), ())), preferred_element_type=F32
    )

    def top(value, back):
        lane = lax.broadcasted_iota(jnp.int32, value.shape, 1)
        if back:
            value = pltpu.roll(value, back, 1)
        return jnp.where(lane == cz - 1, value, 0.0)

    for k in range(ITERS):
        low, high = PAD + (1 + k) * wide, PAD + (tall - 1 - k) * wide
        clear(basis[k], low - 8, low)
        clear(basis[k], high, high + 8)
    for x in range(1, tall - 1):
        given = spread[x * cy : (x + 1) * cy, :]
        extra = jnp.concatenate(
            [top(given[cy - 8 : cy], 1)[8 - HALO : 8], top(given, 0), top(given[0:8], 2)[0:HALO]], axis=0
        )
        here = slice(PAD + x * wide, PAD + (x + 1) * wide)
        basis[0][here, :] = (misfit[here, :] + extra) * inverse[here, :]
    for k in range(1, ITERS + 1):

        def put(x, total, centre):
            here = slice(PAD + x * wide, PAD + (x + 1) * wide)
            basis[k][here, :] = total * inverse[here, :]

        sweep(basis[k - 1], wide, 1 + k, tall - 1 - k, put)

    totals = [jnp.zeros((8, cz), F32) for _ in range(MOMENTS)]
    for x in range(cx):
        at = PAD + (x + HALO) * wide + HALO
        parts = [ref[at : at + cy, :] for ref in basis]
        diagonal = 6.0 + inertia[x]
        scaled = [diagonal * part for part in parts[:ITERS]]
        for m in range(MOMENTS):
            product = scaled[m // 2] * parts[m - m // 2]
            totals[m] = totals[m] + jnp.sum(product.reshape(cy // 8, 8, cz), axis=0)
    lines = [jnp.sum(total, axis=0, keepdims=True) for total in totals]
    lines = jnp.sum(jnp.concatenate(lines, axis=0), axis=1, keepdims=True)
    lane = lax.broadcasted_iota(jnp.int32, (MOMENTS, cz), 1)
    index = lax.broadcasted_iota(jnp.int32, (MOMENTS, cz), 0)
    line = jnp.sum(jnp.where(lane == index, lines, 0.0), axis=0, keepdims=True)
    sums[...] = jnp.broadcast_to(line, sums.shape)


def make_basis(misfit, inverse, inertia, own, left, right, devices):
    cx, cy, cz = inertia.shape
    shape = jax.ShapeDtypeStruct(misfit.shape, F32)
    outs = (shape,) * (ITERS + 1) + (jax.ShapeDtypeStruct((devices, cz), F32),)
    return pl.pallas_call(
        functools.partial(basis_kernel, cx, cy, devices),
        out_shape=outs,
        in_specs=[VMEM] * 6,
        out_specs=(VMEM,) * len(outs),
        scratch_shapes=[pltpu.VMEM((own.shape[1], cz), F32)],
        compiler_params=params(),
        cost_estimate=cost(10**7),
        name="basis",
    )(misfit, inverse, inertia, own, left, right)


def finish_kernel(field, inertia, sums, *refs):
    basis, (state, misfit) = refs[: ITERS + 1], refs[ITERS + 1 :]
    cx, cy, cz = field.shape
    wide = cy + 2 * HALO
    line = jnp.sum(sums[...], axis=0, keepdims=True)
    lane = lax.broadcasted_iota(jnp.int32, line.shape, 1)
    moment = [jnp.sum(jnp.where(lane == m, line, 0.0), axis=1, keepdims=True) for m in range(MOMENTS)]

    def product(a, b):
        total = None
        for m in range(len(a) + len(b) - 1):
            weight = None
            for i in range(len(a)):
                if 0 <= m - i < len(b):
                    term = a[i] * b[m - i]
                    weight = term if weight is None else weight + term
            term = weight * moment[m]
            total = term if total is None else total + term
        return total

    one = jnp.ones((1, 1), F32)
    zero = jnp.zeros((1, 1), F32)
    precond, course, guess = [one], [one], [zero] * ITERS
    norm = moment[0]
    for iteration in range(ITERS):
        image = [a - b for a, b in zip(course + [zero], [zero] + course)]
        multiplier = norm / product(course, image)
        guess = [g + multiplier * c for g, c in zip(guess, course + [zero] * ITERS)]
        precond = [a - multiplier * b for a, b in zip(precond + [zero] * 2, image)]
        if iteration + 1 < ITERS:
            following = product(precond, precond)
            ratio = following / norm
            course = [a + ratio * b for a, b in zip(precond, course + [zero])]
            norm = following
    guess = [jnp.broadcast_to(g, (1, cz)) for g in guess]
    precond = [jnp.broadcast_to(g, (1, cz)) for g in precond]

    for x in range(cx):
        at = PAD + (x + HALO) * wide + HALO
        parts = [ref[at : at + cy, :] for ref in basis]
        value = field[x]
        for g, part in zip(guess, parts):
            value = value + g * part
        state[x] = value
        rest = precond[0] * parts[0]
        for g, part in zip(precond[1:], parts[1:]):
            rest = rest + g * part
        misfit[x] = (6.0 + inertia[x]) * rest


def finish(field, inertia, sums, basis):
    shape = jax.ShapeDtypeStruct(field.shape, F32)
    return pl.pallas_call(
        finish_kernel,
        out_shape=(shape, shape),
        in_specs=[VMEM] * (3 + len(basis)),
        out_specs=(VMEM, VMEM),
        compiler_params=params(),
        cost_estimate=cost(10**6),
        name="finish",
    )(field, inertia, sums, *basis)


def per_device(field, inertia, current, factors, holder, slot):
    count = lax.axis_size("fluid")
    devices = count * lax.axis_size("solid")
    cy = field.shape[1]
    holder = holder.reshape(1, -1)
    slot = slot.reshape(1, -1)

    def swap(value, k):
        return lax.ppermute(value, "fluid", [(i, i ^ k) for i in range(count)])

    blocks = {0: current}
    for k in range(count - 2, 0, -2):
        blocks[k] = swap(current, k)
    near, far = edges(field, inertia, factors, slot, holder)
    near = swap(near, 1)
    outside = [(i, i + 1) for i in range(1, count - 1, 2)] + [(i + 1, i) for i in range(1, count - 1, 2)]
    far = lax.ppermute(far, "fluid", outside)
    for k in range(0, count, 2):
        blocks[k + 1] = swap(blocks[k], 1)
    first, last = sides(field, inertia, near, far)
    left = lax.ppermute(last, "solid", shift("solid", 1))
    right = lax.ppermute(first, "solid", shift("solid", -1))
    own = sources([blocks[k] for k in range(count)], factors, slot, holder, near, far, cy)
    own_left = lax.ppermute(own, "solid", shift("solid", 1))
    own_right = lax.ppermute(own, "solid", shift("solid", -1))
    misfit, inverse = widen(field, inertia, near, far, left, right)
    *basis, sums = make_basis(misfit, inverse, inertia, own, own_left, own_right, devices)
    sums = lax.all_to_all(sums, BOTH, 0, 0, tiled=True)
    return finish(field, inertia, sums, basis)


def solution(mesh):
    return jax.shard_map(
        per_device,
        mesh=mesh,
        in_specs=(
            P("fluid", "solid", None),
            P("fluid", "solid", None),
            P(None, ("fluid", "solid")),
            P(None, ("fluid", "solid")),
            P(("fluid", "solid"), None),
            P(("fluid", "solid")),
        ),
        out_specs=(P("fluid", "solid", None), P("fluid", "solid", None)),
        check_vma=False,
    )
```

time: 62.6 us -> 49.2 us (0.79)
  Pallas kernels: 19.1 us -> 5.88 us
  starting transfers between devices: 23.5 us -> 21.4 us
  blocking collectives: 12.4 us -> 14.3 us
    pallas_call x1, Pallas kernels: 12.3 us -> 1.88 us  [make_basis(): pl.pallas_call(functools.partial(basis_kernel, cx, cy, devices), out_shap...]
    ppermute x2 -> x1, starting transfers between devices: 3.96 us -> 0.79 us  [per_device(): far = lax.ppermute(far, 'fluid', outside)]
    pallas_call x1, Pallas kernels: 3.59 us -> 0.56 us  [widen(): pl.pallas_call(widen_kernel, out_shape=(shape, shape), in_specs=[VMEM] *...]
    all_to_all x1, blocking collectives: 12.4 us -> 14.3 us  [per_device(): sums = lax.all_to_all(sums, BOTH, 0, 0, tiled=True)]
    ppermute x7 -> x8, starting transfers between devices: 8.75 us -> 9.57 us  [swap(): return lax.ppermute(value, 'fluid', [(i, i ^ k) for i in range(count)])]
    ppermute x1, waiting for transfers between devices: 0.01 us -> 0.71 us  [per_device(): own_left = lax.ppermute(own, 'solid', shift('solid', 1))]
    ppermute x7 -> x8, waiting for transfers between devices: 1.82 us -> 1.34 us  [swap(): return lax.ppermute(value, 'fluid', [(i, i ^ k) for i in range(count)])]
    unnamed x22 -> x20, local copies, waits for them, and re-layouts: 4.43 us -> 4.42 us
  transfers between devices with their start and end apart: 13 -> 13, of which waited for: 4 -> 5; matrix products, arithmetic and copies ran while one was open for 0% -> 0% of each run, Pallas kernels for 8% -> 5%
where the time goes in v2:
time: 49.2 us; the launch traced here: 48.8 us
  starting transfers between devices  21.4 us (43%)
  blocking collectives  14.3 us (29%)
  Pallas kernels  5.88 us (12%)
  local copies, waits for them, and re-layouts  4.42 us (9%)
  waiting for transfers between devices  2.06 us (4%)
  between operations  0.8 us (2%)
    all_to_all x1, blocking collectives, per_device(): sums = lax.all_to_all(sums, BOTH, 0, 0, tiled=True)  14.3 us
    ppermute x8, starting transfers between devices, swap(): return lax.ppermute(value, 'fluid', [(i, i ^ k) for i in range(count)])  9.57 us
    ppermute x1, starting transfers between devices, per_device(): own_left = lax.ppermute(own, 'solid', shift('solid', 1))  4.79 us
    unnamed x20, local copies, waits for them, and re-layouts  4.42 us
    ppermute x1, starting transfers between devices, per_device(): left = lax.ppermute(last, 'solid', shift('solid', 1))  3.49 us
    pallas_call x1, Pallas kernels, make_basis(): pl.pallas_call(functools.partial(basis_kernel, cx, cy, devices), out_shap...  1.88 us
    pallas_call x1, Pallas kernels, sources(): pl.pallas_call(functools.partial(source_kernel, count, cy, (HALO - 1) * c...  1.57 us
    ppermute x1, starting transfers between devices, per_device(): right = lax.ppermute(first, 'solid', shift('solid', -1))  1.42 us
  transfers between devices with their start and end apart: 13, of which 5 were waited for; matrix products, arithmetic and copies ran while one was open for 0% of the time, Pallas kernels for 5%

profile of v2, /device:TPU:0, one launch (start us, length us, event | category | flops | bytes accessed | tf_op | source)
XLA Modules:
  0.0 48.8 jit_solution(4282893288220724805)
XLA Ops:
  0.6 0.0 copy-start.7
  0.6 0.7 %copy-done.7 = s32[1024]{0:T(1024)S(1)} copy-done((s32[1024]{0:T(1024)S(1)}, s32[1024]{0:T(1024)}, u32[]{:S(2)}) %copy-start.7) | copy-done | bytes 4120
  1.3 0.0 copy-start
  1.3 1.0 %copy-done = f32[32,32,128]{2,1,0:T(8,128)S(1)} copy-done((f32[32,32,128]{2,1,0:T(8,128)S(1)}, f32[32,32,128]{2,1,0:T(8,128)}, u32[]{:S(2)}) %copy-start) | copy-done | bytes 524312
  2.4 0.0 copy-start.2
  2.4 1.0 %copy-done.2 = f32[32,32,128]{2,1,0:T(8,128)S(1)} copy-done((f32[32,32,128]{2,1,0:T(8,128)S(1)}, f32[32,32,128]{2,1,0:T(8,128)}, u32[]{:S(2)}) %copy-start.2) | copy-done | bytes 524312
  3.4 0.0 copy-start.4
  3.4 0.9 %copy-done.4 = f32[64,1024]{1,0:T(8,128)S(1)} copy-done((f32[64,1024]{1,0:T(8,128)S(1)}, f32[64,1024]{1,0:T(8,128)}, u32[]{:S(2)}) %copy-start.4) | copy-done | bytes 262168
  4.4 0.0 copy-start.8
  4.4 0.7 %copy-done.8 = s32[1024,1]{0,1:T(1,128)S(1)} copy-done((s32[1024,1]{0,1:T(1,128)S(1)}, s32[1024,1]{0,1:T(1,128)}, u32[]{:S(2)}) %copy-start.8) | copy-done | bytes 4120
  5.0 0.0 copy-start.6
  5.0 0.4 edges.1
  5.5 0.6 %collective-permute-start = (f32[296,128]{1,0:T(8,128)S(1)}, f32[296,128]{1,0:T(8,128)S(1)}, u32[]{:S(2)}, u32[]{:S(2)}) collective-permute-start(f32[296,128]{1,0:T(8,128)S(1)} %get-tuple-element.13), channel_id=1, source_target_pairs={{0,4},{4,0},{8,12},{12,8},{16,20},{20,16},{24,28},{28,24},{1,5},{5... | collective-permute-start | bytes 454664 | tf_op jit(solution)/shard_map/ppermute | solution.py:418
  6.0 0.0 copy-start.5
  6.0 0.8 %collective-permute-start.1 = (f32[296,128]{1,0:T(8,128)S(1)}, f32[296,128]{1,0:T(8,128)S(1)}, u32[]{:S(2)}, u32[]{:S(2)}) collective-permute-start(f32[296,128]{1,0:T(8,128)S(1)} %get-tuple-element.14), channel_id=1, source_target_pairs={{4,8},{12,16},{20,24},{8,4},{16,12},{24,20},{5,9},{13,17},{21,25},... | collective-permute-start | bytes 454664 | tf_op jit(solution)/shard_map/ppermute | solution.py:426
  6.8 0.0 copy-done.6
  6.8 5.4 %collective-permute-start.7 = (f32[64,512]{1,0:T(8,128)S(1)}, f32[64,512]{1,0:T(8,128)S(1)}, u32[]{:S(2)}, u32[]{:S(2)}) collective-permute-start(f32[64,512]{1,0:T(8,128)S(1)} %copy-done.6), channel_id=1, source_target_pairs={{0,16},{4,20},{8,24},{12,28},{16,0},{20,4},{24,8},{28,12},{1,17},{... | collective-permute-start | bytes 393224 | tf_op jit(solution)/shard_map/ppermute | solution.py:418
  12.2 0.6 %collective-permute-start.5 = (f32[64,512]{1,0:T(8,128)S(1)}, f32[64,512]{1,0:T(8,128)S(1)}, u32[]{:S(2)}, u32[]{:S(2)}) collective-permute-start(f32[64,512]{1,0:T(8,128)S(1)} %copy-done.6), channel_id=1, source_target_pairs={{0,8},{4,12},{8,0},{12,4},{16,24},{20,28},{24,16},{28,20},{1,9},{5... | collective-permute-start | bytes 393224 | tf_op jit(solution)/shard_map/ppermute | solution.py:418
  12.8 0.0 collective-permute-start.4
  12.8 0.0 collective-permute-done.near.refs_11_
  12.8 0.9 %collective-permute-start.9 = (f32[64,512]{1,0:T(8,128)S(1)}, f32[64,512]{1,0:T(8,128)S(1)}, u32[]{:S(2)}, u32[]{:S(2)}) collective-permute-start(f32[64,512]{1,0:T(8,128)S(1)} %copy-done.6), channel_id=1, source_target_pairs={{0,24},{4,28},{8,16},{12,20},{16,8},{20,12},{24,0},{28,4},{1,25},{... | collective-permute-start | bytes 393224 | tf_op jit(solution)/shard_map/ppermute | solution.py:418
  13.7 0.0 collective-permute-done.1.far.refs_12_
  13.7 0.0 copy-start.9
  13.7 0.1 sides.1
  13.8 3.5 %collective-permute-start.2 = (f32[40,8,128]{2,1,0:T(8,128)S(1)}, f32[40,8,128]{2,1,0:T(8,128)S(1)}, u32[]{:S(2)}, u32[]{:S(2)}) collective-permute-start(f32[40,8,128]{2,1,0:T(8,128)S(1)} %get-tuple-element.15), channel_id=1, source_target_pairs={{0,1},{1,2},{2,3},{4,5},{5,6},{6,7},{8,9},{9,10},{10,11},{12,13},{... | collective-permute-start | bytes 491528 | tf_op jit(solution)/shard_map/ppermute | solution.py:430
  17.3 0.0 collective-permute-done.7.refs_4_
  17.3 0.0 copy-start.1
  17.3 0.0 copy-start.3
  17.3 1.4 %collective-permute-start.3 = (f32[40,8,128]{2,1,0:T(8,128)S(1)}, f32[40,8,128]{2,1,0:T(8,128)S(1)}, u32[]{:S(2)}, u32[]{:S(2)}) collective-permute-start(f32[40,8,128]{2,1,0:T(8,128)S(1)} %get-tuple-element.16), channel_id=1, source_target_pairs={{1,0},{2,1},{3,2},{5,4},{6,5},{7,6},{9,8},{10,9},{11,10},{13,12},{... | collective-permute-start | bytes 491528 | tf_op jit(solution)/shard_map/ppermute | solution.py:431
  18.8 0.0 collective-permute-done.5.refs_2_
  18.8 1.8 %collective-permute-start.8 = (f32[64,512]{1,0:T(8,128)S(1)}, f32[64,512]{1,0:T(8,128)S(1)}, u32[]{:S(2)}, u32[]{:S(2)}) collective-permute-start(f32[64,512]{1,0:T(8,128)S(1)} %collective-permute-done.7.refs_4_), channel_id=1, source_target_pairs={{0,4},{4,0},{8,12},{12,8},{16,20},{20,16},{24,28},{28,24},{1,5},{5... | collective-permute-start | bytes 393224 | tf_op jit(solution)/shard_map/ppermute | solution.py:418
  20.6 0.0 collective-permute-done.4.refs_1_
  20.6 0.1 collective-permute-start.6
  20.7 0.2 collective-permute-done.9.refs_6_
  20.9 0.2 collective-permute-start.10
  21.1 0.5 collective-permute-done.8.refs_5_
  21.6 0.4 collective-permute-done.6.refs_3_
  21.9 0.3 collective-permute-done.10.refs_7_
  22.2 0.0 copy-done.5
  22.2 0.0 copy-done.9
  22.2 1.6 %sources.1.own = f32[1,1280]{1,0:T(1,128)S(1)} custom-call(f32[64,512]{1,0:T(8,128)S(1)} %copy-done.6, f32[64,512]{1,0:T(8,128)S(1)} %collective-permute-done.4.refs_1_, f32[64,512]{1,0:T(8,128)S(1)} %collective-permute-done.5.refs_2_, f32[64,512]{1,0:T(8,128)S(1)} %collective-permute-done.6.refs_3_, f32[64,512]{1,0:T(8,128)S(1)} %collective-permute-done.7.refs_4_, ...), custom_call_target="tpu_custom_call" | custom-call | flops 100000000 | tf_op jit(solution)/shard_map/sources/pallas_call | solution.py:174
  23.8 1.3 %collective-permute-start.12 = (f32[1,1280]{1,0:T(1,128)S(1)}, f32[1,1280]{1,0:T(1,128)S(1)}, u32[]{:S(2)}, u32[]{:S(2)}) collective-permute-start(f32[1,1280]{1,0:T(1,128)S(1)} %sources.1.own), channel_id=1, source_target_pairs={{1,0},{2,1},{3,2},{5,4},{6,5},{7,6},{9,8},{10,9},{11,10},{13,12},{... | collective-permute-start | bytes 15368 | tf_op jit(solution)/shard_map/ppermute | solution.py:434
  25.1 4.8 %collective-permute-start.11 = (f32[1,1280]{1,0:T(1,128)S(1)}, f32[1,1280]{1,0:T(1,128)S(1)}, u32[]{:S(2)}, u32[]{:S(2)}) collective-permute-start(f32[1,1280]{1,0:T(1,128)S(1)} %sources.1.own), channel_id=1, source_target_pairs={{0,1},{1,2},{2,3},{4,5},{5,6},{6,7},{8,9},{9,10},{10,11},{12,13},{... | collective-permute-start | bytes 15368 | tf_op jit(solution)/shard_map/ppermute | solution.py:433
  29.9 0.0 collective-permute-done.2.left
  29.9 0.0 collective-permute-done.3.right
  29.9 0.0 copy-done.1
  29.9 0.0 copy-done.3
  30.0 0.6 %widen.1 = (f32[1616,128]{1,0:T(8,128)S(1)}, f32[1616,128]{1,0:T(8,128)S(1)}) custom-call(f32[32,32,128]{2,1,0:T(8,128)S(1)} %copy-done.3, f32[32,32,128]{2,1,0:T(8,128)S(1)} %copy-done.1, f32[296,128]{1,0:T(8,128)S(1)} %collective-permute-done.near.refs_11_, f32[296,128]{1,0:T(8,128)S(1)} %collective-permute-done.1.far.refs_12_, ...), custom_call_target="tpu_custom_call" | custom-call | flops 10000000 | tf_op jit(solution)/shard_map/widen/pallas_call | solution.py:258
  30.5 0.0 collective-permute-done.12.right
  30.5 0.7 %collective-permute-done.11.left = f32[1,1280]{1,0:T(1,128)S(1)} collective-permute-done((f32[1,1280]{1,0:T(1,128)S(1)}, f32[1,1280]{1,0:T(1,128)S(1)}, u32[]{:S(2)}, u32[]{:S(2)}) %collective-permute-start.11) | collective-permute-done | bytes 5152 | tf_op jit(solution)/shard_map/ppermute | solution.py:433
  31.2 1.9 %basis.1 = (f32[1616,128]{1,0:T(8,128)S(1)}, f32[1616,128]{1,0:T(8,128)S(1)}, f32[1616,128]{1,0:T(8,128)S(1)}, f32[1616,128]{1,0:T(8,128)S(1)}, f32[32,128]{1,0:T(8,128)S(1)}) custom-call(f32[1616,128]{1,0:T(8,128)S(1)} %get-tuple-element.17.misfit, f32[1616,128]{1,0:T(8,128)S(1)} %get-tuple-element.18.inverse, f32[32,32,128]{2,1,0:T(8,128)S(1)} %copy-done.1, ...), custom_call_target="tpu_custom_call" | custom-call | flops 10000000 | tf_op jit(solution)/shard_map/basis/pallas_call | solution.py:335
  33.1 14.3 %all_to_all.11 = f32[32,1,128]{2,1,0:T(1,128)S(1)} all-to-all(f32[32,1,128]{2,1,0:T(1,128)S(1)} %bitcast.15), channel_id=1, replica_groups=mesh['fluid'=8,'solid'=4] {'fluid','solid'}, dimensions={0} | all-to-all | bytes 32768 | tf_op jit(solution)/shard_map/all_to_all | solution.py:437
  47.4 1.4 %finish.1 = (f32[32,32,128]{2,1,0:T(8,128)}, f32[32,32,128]{2,1,0:T(8,128)}) custom-call(f32[32,32,128]{2,1,0:T(8,128)S(1)} %copy-done.3, f32[32,32,128]{2,1,0:T(8,128)S(1)} %copy-done.1, f32[32,128]{1,0:T(8,128)S(1)} %bitcast.10, f32[1616,128]{1,0:T(8,128)S(1)} %get-tuple-element.20.refs_0_, f32[1616,128]{1,0:T(8,128)S(1)} %get-tuple-element.21.refs_1_, ...), custom_call_target="tpu_custom_call" | custom-call | flops 1000000 | tf_op jit(solution)/shard_map/finish/pallas_call | solution.py:399
Async XLA Ops:
  0.6 0.7 %copy-start.7 = (s32[1024]{0:T(1024)S(1)}, s32[1024]{0:T(1024)}, u32[]{:S(2)}) copy-start(s32[1024]{0:T(1024)} %param.11) | copy-start | bytes 12292
  1.3 1.0 %copy-start = (f32[32,32,128]{2,1,0:T(8,128)S(1)}, f32[32,32,128]{2,1,0:T(8,128)}, u32[]{:S(2)}) copy-start(f32[32,32,128]{2,1,0:T(8,128)} %inertia.7) | copy-start | bytes 1572868
  2.4 1.0 %copy-start.2 = (f32[32,32,128]{2,1,0:T(8,128)S(1)}, f32[32,32,128]{2,1,0:T(8,128)}, u32[]{:S(2)}) copy-start(f32[32,32,128]{2,1,0:T(8,128)} %field.5) | copy-start | bytes 1572868
  3.4 0.9 %copy-start.4 = (f32[64,1024]{1,0:T(8,128)S(1)}, f32[64,1024]{1,0:T(8,128)}, u32[]{:S(2)}) copy-start(f32[64,1024]{1,0:T(8,128)} %refs_8_.1) | copy-start | bytes 786436
  4.4 0.7 %copy-start.8 = (s32[1024,1]{0,1:T(1,128)S(1)}, s32[1024,1]{0,1:T(1,128)}, u32[]{:S(2)}) copy-start(s32[1024,1]{0,1:T(1,128)} %param.10) | copy-start | bytes 12292
  5.0 1.8 %copy-start.6 = (f32[64,512]{1,0:T(8,128)S(1)}, f32[64,512]{1,0:T(8,128)}, u32[]{:S(2)}) copy-start(f32[64,512]{1,0:T(8,128)} %refs_0_.1) | copy-start | bytes 393220
  5.5 7.3 %collective-permute-start = (f32[296,128]{1,0:T(8,128)S(1)}, f32[296,128]{1,0:T(8,128)S(1)}, u32[]{:S(2)}, u32[]{:S(2)}) collective-permute-start(f32[296,128]{1,0:T(8,128)S(1)} %get-tuple-element.13), channel_id=1, source_target_pairs={{0,4},{4,0},{8,12},{12,8},{16,20},{20,16},{24,28},{28,24},{1,5},{5... | collective-permute-start | bytes 454664 | tf_op jit(solution)/shard_map/ppermute | solution.py:418
  6.0 16.2 %copy-start.5 = (f32[64,1024]{1,0:T(8,128)S(1)}, f32[64,1024]{1,0:T(8,128)}, u32[]{:S(2)}) copy-start(f32[64,1024]{1,0:T(8,128)} %refs_8_.1) | copy-start | bytes 786436
  6.0 7.7 %collective-permute-start.1 = (f32[296,128]{1,0:T(8,128)S(1)}, f32[296,128]{1,0:T(8,128)S(1)}, u32[]{:S(2)}, u32[]{:S(2)}) collective-permute-start(f32[296,128]{1,0:T(8,128)S(1)} %get-tuple-element.14), channel_id=1, source_target_pairs={{4,8},{12,16},{20,24},{8,4},{16,12},{24,20},{5,9},{13,17},{21,25},... | collective-permute-start | bytes 454664 | tf_op jit(solution)/shard_map/ppermute | solution.py:426
  6.8 10.5 %collective-permute-start.7 = (f32[64,512]{1,0:T(8,128)S(1)}, f32[64,512]{1,0:T(8,128)S(1)}, u32[]{:S(2)}, u32[]{:S(2)}) collective-permute-start(f32[64,512]{1,0:T(8,128)S(1)} %copy-done.6), channel_id=1, source_target_pairs={{0,16},{4,20},{8,24},{12,28},{16,0},{20,4},{24,8},{28,12},{1,17},{... | collective-permute-start | bytes 393224 | tf_op jit(solution)/shard_map/ppermute | solution.py:418
  12.2 6.6 %collective-permute-start.5 = (f32[64,512]{1,0:T(8,128)S(1)}, f32[64,512]{1,0:T(8,128)S(1)}, u32[]{:S(2)}, u32[]{:S(2)}) collective-permute-start(f32[64,512]{1,0:T(8,128)S(1)} %copy-done.6), channel_id=1, source_target_pairs={{0,8},{4,12},{8,0},{12,4},{16,24},{20,28},{24,16},{28,20},{1,9},{5... | collective-permute-start | bytes 393224 | tf_op jit(solution)/shard_map/ppermute | solution.py:418
  12.8 7.8 %collective-permute-start.4 = (f32[64,512]{1,0:T(8,128)S(1)}, f32[64,512]{1,0:T(8,128)S(1)}, u32[]{:S(2)}, u32[]{:S(2)}) collective-permute-start(f32[64,512]{1,0:T(8,128)S(1)} %copy-done.6), channel_id=1, source_target_pairs={{0,4},{4,0},{8,12},{12,8},{16,20},{20,16},{24,28},{28,24},{1,5},{5... | collective-permute-start | bytes 393224 | tf_op jit(solution)/shard_map/ppermute | solution.py:418
  12.8 8.1 %collective-permute-start.9 = (f32[64,512]{1,0:T(8,128)S(1)}, f32[64,512]{1,0:T(8,128)S(1)}, u32[]{:S(2)}, u32[]{:S(2)}) collective-permute-start(f32[64,512]{1,0:T(8,128)S(1)} %copy-done.6), channel_id=1, source_target_pairs={{0,24},{4,28},{8,16},{12,20},{16,8},{20,12},{24,0},{28,4},{1,25},{... | collective-permute-start | bytes 393224 | tf_op jit(solution)/shard_map/ppermute | solution.py:418
  13.7 8.5 %copy-start.9 = (s32[1024,1]{0,1:T(1,128)S(1)}, s32[1024,1]{0,1:T(1,128)}, u32[]{:S(2)}) copy-start(s32[1024,1]{0,1:T(1,128)} %param.10) | copy-start | bytes 12292
  13.8 16.1 %collective-permute-start.2 = (f32[40,8,128]{2,1,0:T(8,128)S(1)}, f32[40,8,128]{2,1,0:T(8,128)S(1)}, u32[]{:S(2)}, u32[]{:S(2)}) collective-permute-start(f32[40,8,128]{2,1,0:T(8,128)S(1)} %get-tuple-element.15), channel_id=1, source_target_pairs={{0,1},{1,2},{2,3},{4,5},{5,6},{6,7},{8,9},{9,10},{10,11},{12,13},{... | collective-permute-start | bytes 491528 | tf_op jit(solution)/shard_map/ppermute | solution.py:430
  17.3 12.6 %copy-start.1 = (f32[32,32,128]{2,1,0:T(8,128)S(1)}, f32[32,32,128]{2,1,0:T(8,128)}, u32[]{:S(2)}) copy-start(f32[32,32,128]{2,1,0:T(8,128)} %inertia.7) | copy-start | bytes 1572868
  17.3 12.6 %copy-start.3 = (f32[32,32,128]{2,1,0:T(8,128)S(1)}, f32[32,32,128]{2,1,0:T(8,128)}, u32[]{:S(2)}) copy-start(f32[32,32,128]{2,1,0:T(8,128)} %field.5) | copy-start | bytes 1572868
  17.3 12.6 %collective-permute-start.3 = (f32[40,8,128]{2,1,0:T(8,128)S(1)}, f32[40,8,128]{2,1,0:T(8,128)S(1)}, u32[]{:S(2)}, u32[]{:S(2)}) collective-permute-start(f32[40,8,128]{2,1,0:T(8,128)S(1)} %get-tuple-element.16), channel_id=1, source_target_pairs={{1,0},{2,1},{3,2},{5,4},{6,5},{7,6},{9,8},{10,9},{11,10},{13,12},{... | collective-permute-start | bytes 491528 | tf_op jit(solution)/shard_map/ppermute | solution.py:431
  18.8 2.8 %collective-permute-start.8 = (f32[64,512]{1,0:T(8,128)S(1)}, f32[64,512]{1,0:T(8,128)S(1)}, u32[]{:S(2)}, u32[]{:S(2)}) collective-permute-start(f32[64,512]{1,0:T(8,128)S(1)} %collective-permute-done.7.refs_4_), channel_id=1, source_target_pairs={{0,4},{4,0},{8,12},{12,8},{16,20},{20,16},{24,28},{28,24},{1,5},{5... | collective-permute-start | bytes 393224 | tf_op jit(solution)/shard_map/ppermute | solution.py:418
  20.6 1.3 %collective-permute-start.6 = (f32[64,512]{1,0:T(8,128)S(1)}, f32[64,512]{1,0:T(8,128)S(1)}, u32[]{:S(2)}, u32[]{:S(2)}) collective-permute-start(f32[64,512]{1,0:T(8,128)S(1)} %collective-permute-done.5.refs_2_), channel_id=1, source_target_pairs={{0,4},{4,0},{8,12},{12,8},{16,20},{20,16},{24,28},{28,24},{1,5},{5... | collective-permute-start | bytes 393224 | tf_op jit(solution)/shard_map/ppermute | solution.py:418
  20.9 1.3 %collective-permute-start.10 = (f32[64,512]{1,0:T(8,128)S(1)}, f32[64,512]{1,0:T(8,128)S(1)}, u32[]{:S(2)}, u32[]{:S(2)}) collective-permute-start(f32[64,512]{1,0:T(8,128)S(1)} %collective-permute-done.9.refs_6_), channel_id=1, source_target_pairs={{0,4},{4,0},{8,12},{12,8},{16,20},{20,16},{24,28},{28,24},{1,5},{5... | collective-permute-start | bytes 393224 | tf_op jit(solution)/shard_map/ppermute | solution.py:418
  23.8 6.7 %collective-permute-start.12 = (f32[1,1280]{1,0:T(1,128)S(1)}, f32[1,1280]{1,0:T(1,128)S(1)}, u32[]{:S(2)}, u32[]{:S(2)}) collective-permute-start(f32[1,1280]{1,0:T(1,128)S(1)} %sources.1.own), channel_id=1, source_target_pairs={{1,0},{2,1},{3,2},{5,4},{6,5},{7,6},{9,8},{10,9},{11,10},{13,12},{... | collective-permute-start | bytes 15368 | tf_op jit(solution)/shard_map/ppermute | solution.py:434
  25.1 6.1 %collective-permute-start.11 = (f32[1,1280]{1,0:T(1,128)S(1)}, f32[1,1280]{1,0:T(1,128)S(1)}, u32[]{:S(2)}, u32[]{:S(2)}) collective-permute-start(f32[1,1280]{1,0:T(1,128)S(1)} %sources.1.own), channel_id=1, source_target_pairs={{0,1},{1,2},{2,3},{4,5},{5,6},{6,7},{8,9},{9,10},{10,11},{12,13},{... | collective-permute-start | bytes 15368 | tf_op jit(solution)/shard_map/ppermute | solution.py:433

commit v3 on v2

--- a/solution.py
+++ b/solution.py
@@ -27,9 +27,7 @@
 
 def shift(axis, step):
     size = lax.axis_size(axis)
-    if step > 0:
-        return [(i, i + 1) for i in range(size - 1)]
-    return [(i + 1, i) for i in range(size - 1)]
+    return [(i, (i + step) % size) for i in range(size)]
 
 
 def even():
@@ -72,6 +70,7 @@
     edge = HALO * cy
     length = edge + (HALO - 1) * cy + factors.shape[0] + 8
     shape = jax.ShapeDtypeStruct((length, cz), F32)
+    operands = (field.reshape(cx * cy, cz), inertia.reshape(cx * cy, cz), factors, slot, holder)
     return pl.pallas_call(
         functools.partial(edge_kernel, cy),
         out_shape=(shape, shape),
@@ -81,7 +80,7 @@
         compiler_params=params(),
         cost_estimate=cost(10**5),
         name="edges",
-    )(field.reshape(cx * cy, cz), inertia.reshape(cx * cy, cz), factors, slot, holder)
+    )(*(pltpu.with_memory_space_constraint(t, pltpu.HBM) for t in operands))
 
 
 def side_kernel(field, inertia, near, far, first, last):
@@ -218,6 +217,9 @@
     wide = cy + 2 * HALO
     tall = cx + 2 * HALO
     is_even = even()
+    i, j = lax.axis_index("fluid"), lax.axis_index("solid")
+    has_below, has_above = i > 0, i < lax.axis_size("fluid") - 1
+    has_left, has_right = j > 0, j < lax.axis_size("solid") - 1
     clear(wide_field, 0, PAD)
     clear(wide_field, PAD + tall * wide, 2 * PAD + tall * wide)
     none = jnp.zeros((1, cz), F32)
@@ -237,7 +239,13 @@
             middle = ends(near, far, at, at + cy)
             at = edge + at
             capacity = ends(near, far, at, at + cy) if x < tall - 1 else None
-        before, after = left[x], right[x]
+        before = jnp.where(has_left, left[x], 0.0)
+        after = jnp.where(has_right, right[x], 0.0)
+        if not HALO <= x < cx + HALO:
+            inside = has_below if x < HALO else has_above
+            before, middle, after = (jnp.where(inside, t, 0.0) for t in (before, middle, after))
+            if capacity is not None:
+                capacity = jnp.where(inside, capacity, 0.0)
         here = slice(PAD + x * wide, PAD + (x + 1) * wide)
         wide_field[here, :] = jnp.concatenate([before[0:HALO], middle, after[0:HALO]], axis=0)
         if capacity is not None:
@@ -422,8 +430,7 @@
         blocks[k] = swap(current, k)
     near, far = edges(field, inertia, factors, slot, holder)
     near = swap(near, 1)
-    outside = [(i, i + 1) for i in range(1, count - 1, 2)] + [(i + 1, i) for i in range(1, count - 1, 2)]
-    far = lax.ppermute(far, "fluid", outside)
+    far = lax.ppermute(far, "fluid", [(i, (i + 2 * (i % 2) - 1) % count) for i in range(count)])
     for k in range(0, count, 2):
         blocks[k + 1] = swap(blocks[k], 1)
     first, last = sides(field, inertia, near, far)

time: 49.2 us -> 40.6 us (0.83)
  blocking collectives: 14.3 us -> 8.92 us
  waiting for transfers between devices: 2.06 us -> 7.04 us
  local copies, waits for them, and re-layouts: 4.42 us -> 0.02 us
  starting transfers between devices: 21.4 us -> 17.1 us
  Pallas kernels: 5.88 us -> 6.69 us
    all_to_all x1, blocking collectives: 14.3 us -> 8.92 us  [per_device(): sums = lax.all_to_all(sums, BOTH, 0, 0, tiled=True)]
    ppermute x8, starting transfers between devices: 9.57 us -> 4.56 us  [swap(): return lax.ppermute(value, 'fluid', [(i, i ^ k) for i in range(count)])]
    ppermute x1, starting transfers between devices: 4.79 us -> 0.01 us  [per_device(): own_left = lax.ppermute(own, 'solid', shift('solid', 1))]
    unnamed x20 -> x12, local copies, waits for them, and re-layouts: 4.42 us -> 0.02 us
    ppermute x1, waiting for transfers between devices: 0.71 us -> 4.08 us  [per_device(): own_left = lax.ppermute(own, 'solid', shift('solid', 1))]
    ppermute x1, starting transfers between devices: 0.79 us -> 3.54 us  [per_device(): lax.ppermute(far, 'fluid', [(i, (i + 2 * (i % 2) - 1) % count) for i in r...]
    ppermute x1, starting transfers between devices: 1.29 us -> 3.82 us  [per_device(): own_right = lax.ppermute(own, 'solid', shift('solid', -1))]
    ppermute x1, starting transfers between devices: 1.42 us -> 3.54 us  [per_device(): right = lax.ppermute(first, 'solid', shift('solid', -1))]
  transfers between devices with their start and end apart: 13 -> 13, of which waited for: 5 -> 7; matrix products, arithmetic and copies ran while one was open for 0% -> 0% of each run, Pallas kernels for 5% -> 5%
where the time goes in v3:
time: 40.6 us; the launch traced here: 40.5 us
  starting transfers between devices  17.1 us (42%)
  blocking collectives  8.92 us (22%)
  waiting for transfers between devices  7.04 us (17%)
  Pallas kernels  6.69 us (16%)
  between operations  0.71 us (2%)
    all_to_all x1, blocking collectives, per_device(): sums = lax.all_to_all(sums, BOTH, 0, 0, tiled=True)  8.92 us
    ppermute x8, starting transfers between devices, swap(): return lax.ppermute(value, 'fluid', [(i, i ^ k) for i in range(count)])  4.56 us
    ppermute x1, waiting for transfers between devices, per_device(): own_left = lax.ppermute(own, 'solid', shift('solid', 1))  4.08 us
    ppermute x1, starting transfers between devices, per_device(): own_right = lax.ppermute(own, 'solid', shift('solid', -1))  3.82 us
    ppermute x1, starting transfers between devices, per_device(): lax.ppermute(far, 'fluid', [(i, (i + 2 * (i % 2) - 1) % count) for i in r...  3.54 us
    ppermute x1, starting transfers between devices, per_device(): right = lax.ppermute(first, 'solid', shift('solid', -1))  3.54 us
    pallas_call x1, Pallas kernels, make_basis(): pl.pallas_call(functools.partial(basis_kernel, cx, cy, devices), out_shap...  1.92 us
    ppermute x1, starting transfers between devices, per_device(): left = lax.ppermute(last, 'solid', shift('solid', 1))  1.63 us
  transfers between devices with their start and end apart: 13, of which 7 were waited for; matrix products, arithmetic and copies ran while one was open for 0% of the time, Pallas kernels for 5%

profile of v3, /device:TPU:0, one launch (start us, length us, event | category | flops | bytes accessed | tf_op | source)
XLA Modules:
  0.0 40.5 jit_solution(9720859777523257738)
XLA Ops:
  0.6 0.0 copy-start.3
  0.6 0.0 copy-start
  0.6 0.0 copy-start.1
  0.7 1.1 %edges.1 = (f32[296,128]{1,0:T(8,128)S(1)}, f32[296,128]{1,0:T(8,128)S(1)}) custom-call(f32[1024,128]{1,0:T(8,128)} %bitcast.9, f32[1024,128]{1,0:T(8,128)} %bitcast.8, f32[64,1024]{1,0:T(8,128)} %refs_8_.1, s32[1,1024]{1,0:T(1,128)} %bitcast.11, s32[1,1024]{1,0:T(1,128)} %bitcast.13), custom_call_target="tpu_custom_call" | custom-call | flops 100000 | tf_op jit(solution)/shard_map/edges/pallas_call | solution.py:74
  1.8 0.6 %collective-permute-start = (f32[296,128]{1,0:T(8,128)S(1)}, f32[296,128]{1,0:T(8,128)S(1)}, u32[]{:S(2)}, u32[]{:S(2)}) collective-permute-start(f32[296,128]{1,0:T(8,128)S(1)} %get-tuple-element.13), channel_id=1, source_target_pairs={{0,4},{4,0},{8,12},{12,8},{16,20},{20,16},{24,28},{28,24},{1,5},{5... | collective-permute-start | bytes 454664 | tf_op jit(solution)/shard_map/ppermute | solution.py:426
  2.4 0.0 copy-start.2
  2.4 3.5 %collective-permute-start.1 = (f32[296,128]{1,0:T(8,128)S(1)}, f32[296,128]{1,0:T(8,128)S(1)}, u32[]{:S(2)}, u32[]{:S(2)}) collective-permute-start(f32[296,128]{1,0:T(8,128)S(1)} %get-tuple-element.14), channel_id=1, source_target_pairs={{0,28},{4,8},{8,4},{12,16},{16,12},{20,24},{24,20},{28,0},{1,29},{... | collective-permute-start | bytes 454664 | tf_op jit(solution)/shard_map/ppermute | solution.py:433
  5.9 0.0 copy-done.3
  5.9 0.5 %collective-permute-start.7 = (f32[64,512]{1,0:T(8,128)S(1)}, f32[64,512]{1,0:T(8,128)S(1)}, u32[]{:S(2)}, u32[]{:S(2)}) collective-permute-start(f32[64,512]{1,0:T(8,128)S(1)} %copy-done.3), channel_id=1, source_target_pairs={{0,16},{4,20},{8,24},{12,28},{16,0},{20,4},{24,8},{28,12},{1,17},{... | collective-permute-start | bytes 393224 | tf_op jit(solution)/shard_map/ppermute | solution.py:426
  6.4 0.6 %collective-permute-start.5 = (f32[64,512]{1,0:T(8,128)S(1)}, f32[64,512]{1,0:T(8,128)S(1)}, u32[]{:S(2)}, u32[]{:S(2)}) collective-permute-start(f32[64,512]{1,0:T(8,128)S(1)} %copy-done.3), channel_id=1, source_target_pairs={{0,8},{4,12},{8,0},{12,4},{16,24},{20,28},{24,16},{28,20},{1,9},{5... | collective-permute-start | bytes 393224 | tf_op jit(solution)/shard_map/ppermute | solution.py:426
  7.0 0.0 collective-permute-start.4
  7.0 0.0 collective-permute-done.near.refs_11_
  7.0 2.4 %collective-permute-start.9 = (f32[64,512]{1,0:T(8,128)S(1)}, f32[64,512]{1,0:T(8,128)S(1)}, u32[]{:S(2)}, u32[]{:S(2)}) collective-permute-start(f32[64,512]{1,0:T(8,128)S(1)} %copy-done.3), channel_id=1, source_target_pairs={{0,24},{4,28},{8,16},{12,20},{16,8},{20,12},{24,0},{28,4},{1,25},{... | collective-permute-start | bytes 393224 | tf_op jit(solution)/shard_map/ppermute | solution.py:426
  9.4 0.7 %collective-permute-done.1.far.refs_12_ = f32[296,128]{1,0:T(8,128)S(1)} collective-permute-done((f32[296,128]{1,0:T(8,128)S(1)}, f32[296,128]{1,0:T(8,128)S(1)}, u32[]{:S(2)}, u32[]{:S(2)}) %collective-permute-start.1) | collective-permute-done | bytes 151584 | tf_op jit(solution)/shard_map/ppermute | solution.py:433
  10.1 0.0 copy-done
  10.1 0.0 copy-done.1
  10.1 0.0 copy-start.4
  10.1 0.0 copy-start.5
  10.1 0.1 sides.1
  10.2 1.6 %collective-permute-start.2 = (f32[40,8,128]{2,1,0:T(8,128)S(1)}, f32[40,8,128]{2,1,0:T(8,128)S(1)}, u32[]{:S(2)}, u32[]{:S(2)}) collective-permute-start(f32[40,8,128]{2,1,0:T(8,128)S(1)} %get-tuple-element.15), channel_id=1, source_target_pairs={{0,1},{1,2},{2,3},{3,0},{4,5},{5,6},{6,7},{7,4},{8,9},{9,10},{10,1... | collective-permute-start | bytes 491528 | tf_op jit(solution)/shard_map/ppermute | solution.py:437
  11.8 0.0 collective-permute-done.7.refs_4_
  11.8 3.5 %collective-permute-start.3 = (f32[40,8,128]{2,1,0:T(8,128)S(1)}, f32[40,8,128]{2,1,0:T(8,128)S(1)}, u32[]{:S(2)}, u32[]{:S(2)}) collective-permute-start(f32[40,8,128]{2,1,0:T(8,128)S(1)} %get-tuple-element.16), channel_id=1, source_target_pairs={{0,3},{1,0},{2,1},{3,2},{4,7},{5,4},{6,5},{7,6},{8,11},{9,8},{10,9... | collective-permute-start | bytes 491528 | tf_op jit(solution)/shard_map/ppermute | solution.py:438
  15.4 0.0 collective-permute-done.5.refs_2_
  15.4 0.0 collective-permute-start.8
  15.4 0.0 collective-permute-done.4.refs_1_
  15.4 0.5 %collective-permute-start.6 = (f32[64,512]{1,0:T(8,128)S(1)}, f32[64,512]{1,0:T(8,128)S(1)}, u32[]{:S(2)}, u32[]{:S(2)}) collective-permute-start(f32[64,512]{1,0:T(8,128)S(1)} %collective-permute-done.5.refs_2_), channel_id=1, source_target_pairs={{0,4},{4,0},{8,12},{12,8},{16,20},{20,16},{24,28},{28,24},{1,5},{5... | collective-permute-start | bytes 393224 | tf_op jit(solution)/shard_map/ppermute | solution.py:426
  15.9 0.1 collective-permute-done.9.refs_6_
  16.0 0.0 collective-permute-start.10
  16.0 0.7 %collective-permute-done.8.refs_5_ = f32[64,512]{1,0:T(8,128)S(1)} collective-permute-done((f32[64,512]{1,0:T(8,128)S(1)}, f32[64,512]{1,0:T(8,128)S(1)}, u32[]{:S(2)}, u32[]{:S(2)}) %collective-permute-start.8) | collective-permute-done | bytes 131104 | tf_op jit(solution)/shard_map/ppermute | solution.py:426
  16.7 0.2 collective-permute-done.6.refs_3_
  16.9 0.5 %collective-permute-done.10.refs_7_ = f32[64,512]{1,0:T(8,128)S(1)} collective-permute-done((f32[64,512]{1,0:T(8,128)S(1)}, f32[64,512]{1,0:T(8,128)S(1)}, u32[]{:S(2)}, u32[]{:S(2)}) %collective-permute-start.10) | collective-permute-done | bytes 131104 | tf_op jit(solution)/shard_map/ppermute | solution.py:426
  17.4 0.0 copy-done.2
  17.4 0.0 copy-done.4
  17.4 0.0 copy-done.5
  17.4 1.6 %sources.1.own = f32[1,1280]{1,0:T(1,128)S(1)} custom-call(f32[64,512]{1,0:T(8,128)S(1)} %copy-done.3, f32[64,512]{1,0:T(8,128)S(1)} %collective-permute-done.4.refs_1_, f32[64,512]{1,0:T(8,128)S(1)} %collective-permute-done.5.refs_2_, f32[64,512]{1,0:T(8,128)S(1)} %collective-permute-done.6.refs_3_, f32[64,512]{1,0:T(8,128)S(1)} %collective-permute-done.7.refs_4_, ...), custom_call_target="tpu_custom_call" | custom-call | flops 100000000 | tf_op jit(solution)/shard_map/sources/pallas_call | solution.py:173
  19.0 3.8 %collective-permute-start.12 = (f32[1,1280]{1,0:T(1,128)S(1)}, f32[1,1280]{1,0:T(1,128)S(1)}, u32[]{:S(2)}, u32[]{:S(2)}) collective-permute-start(f32[1,1280]{1,0:T(1,128)S(1)} %sources.1.own), channel_id=1, source_target_pairs={{0,3},{1,0},{2,1},{3,2},{4,7},{5,4},{6,5},{7,6},{8,11},{9,8},{10,9... | collective-permute-start | bytes 15368 | tf_op jit(solution)/shard_map/ppermute | solution.py:441
  22.8 0.0 collective-permute-start.11
  22.8 0.0 collective-permute-done.2.left
  22.8 0.0 collective-permute-done.3.right
  22.8 0.5 %widen.1 = (f32[1616,128]{1,0:T(8,128)S(1)}, f32[1616,128]{1,0:T(8,128)S(1)}) custom-call(f32[32,32,128]{2,1,0:T(8,128)S(1)} %copy-done.1, f32[32,32,128]{2,1,0:T(8,128)S(1)} %copy-done, f32[296,128]{1,0:T(8,128)S(1)} %collective-permute-done.near.refs_11_, f32[296,128]{1,0:T(8,128)S(1)} %collective-permute-done.1.far.refs_12_, ...), custom_call_target="tpu_custom_call" | custom-call | flops 10000000 | tf_op jit(solution)/shard_map/widen/pallas_call | solution.py:266
  23.4 0.8 %collective-permute-done.12.right = f32[1,1280]{1,0:T(1,128)S(1)} collective-permute-done((f32[1,1280]{1,0:T(1,128)S(1)}, f32[1,1280]{1,0:T(1,128)S(1)}, u32[]{:S(2)}, u32[]{:S(2)}) %collective-permute-start.12) | collective-permute-done | bytes 5152 | tf_op jit(solution)/shard_map/ppermute | solution.py:441
  24.1 4.1 %collective-permute-done.11.left = f32[1,1280]{1,0:T(1,128)S(1)} collective-permute-done((f32[1,1280]{1,0:T(1,128)S(1)}, f32[1,1280]{1,0:T(1,128)S(1)}, u32[]{:S(2)}, u32[]{:S(2)}) %collective-permute-start.11) | collective-permute-done | bytes 5152 | tf_op jit(solution)/shard_map/ppermute | solution.py:440
  28.2 1.9 %basis.1 = (f32[1616,128]{1,0:T(8,128)S(1)}, f32[1616,128]{1,0:T(8,128)S(1)}, f32[1616,128]{1,0:T(8,128)S(1)}, f32[1616,128]{1,0:T(8,128)S(1)}, f32[32,128]{1,0:T(8,128)S(1)}) custom-call(f32[1616,128]{1,0:T(8,128)S(1)} %get-tuple-element.17.misfit, f32[1616,128]{1,0:T(8,128)S(1)} %get-tuple-element.18.inverse, f32[32,32,128]{2,1,0:T(8,128)S(1)} %copy-done, ...), custom_call_target="tpu_custom_call" | custom-call | flops 10000000 | tf_op jit(solution)/shard_map/basis/pallas_call | solution.py:343
  30.1 8.9 %all_to_all.11 = f32[32,1,128]{2,1,0:T(1,128)S(1)} all-to-all(f32[32,1,128]{2,1,0:T(1,128)S(1)} %bitcast.15), channel_id=1, replica_groups=mesh['fluid'=8,'solid'=4] {'fluid','solid'}, dimensions={0} | all-to-all | bytes 32768 | tf_op jit(solution)/shard_map/all_to_all | solution.py:444
  39.0 1.4 %finish.1 = (f32[32,32,128]{2,1,0:T(8,128)}, f32[32,32,128]{2,1,0:T(8,128)}) custom-call(f32[32,32,128]{2,1,0:T(8,128)S(1)} %copy-done.1, f32[32,32,128]{2,1,0:T(8,128)S(1)} %copy-done, f32[32,128]{1,0:T(8,128)S(1)} %bitcast.10, f32[1616,128]{1,0:T(8,128)S(1)} %get-tuple-element.20.refs_0_, f32[1616,128]{1,0:T(8,128)S(1)} %get-tuple-element.21.refs_1_, ...), custom_call_target="tpu_custom_call" | custom-call | flops 1000000 | tf_op jit(solution)/shard_map/finish/pallas_call | solution.py:407
Async XLA Ops:
  0.6 5.3 %copy-start.3 = (f32[64,512]{1,0:T(8,128)S(1)}, f32[64,512]{1,0:T(8,128)}, u32[]{:S(2)}) copy-start(f32[64,512]{1,0:T(8,128)} %refs_0_.1) | copy-start | bytes 393220
  0.6 9.5 %copy-start = (f32[32,32,128]{2,1,0:T(8,128)S(1)}, f32[32,32,128]{2,1,0:T(8,128)}, u32[]{:S(2)}) copy-start(f32[32,32,128]{2,1,0:T(8,128)} %inertia.7) | copy-start | bytes 1572868
  0.6 9.5 %copy-start.1 = (f32[32,32,128]{2,1,0:T(8,128)S(1)}, f32[32,32,128]{2,1,0:T(8,128)}, u32[]{:S(2)}) copy-start(f32[32,32,128]{2,1,0:T(8,128)} %field.5) | copy-start | bytes 1572868
  1.8 5.2 %collective-permute-start = (f32[296,128]{1,0:T(8,128)S(1)}, f32[296,128]{1,0:T(8,128)S(1)}, u32[]{:S(2)}, u32[]{:S(2)}) collective-permute-start(f32[296,128]{1,0:T(8,128)S(1)} %get-tuple-element.13), channel_id=1, source_target_pairs={{0,4},{4,0},{8,12},{12,8},{16,20},{20,16},{24,28},{28,24},{1,5},{5... | collective-permute-start | bytes 454664 | tf_op jit(solution)/shard_map/ppermute | solution.py:426
  2.4 15.0 %copy-start.2 = (f32[64,1024]{1,0:T(8,128)S(1)}, f32[64,1024]{1,0:T(8,128)}, u32[]{:S(2)}) copy-start(f32[64,1024]{1,0:T(8,128)} %refs_8_.1) | copy-start | bytes 786436
  2.4 7.7 %collective-permute-start.1 = (f32[296,128]{1,0:T(8,128)S(1)}, f32[296,128]{1,0:T(8,128)S(1)}, u32[]{:S(2)}, u32[]{:S(2)}) collective-permute-start(f32[296,128]{1,0:T(8,128)S(1)} %get-tuple-element.14), channel_id=1, source_target_pairs={{0,28},{4,8},{8,4},{12,16},{16,12},{20,24},{24,20},{28,0},{1,29},{... | collective-permute-start | bytes 454664 | tf_op jit(solution)/shard_map/ppermute | solution.py:433
  5.9 5.9 %collective-permute-start.7 = (f32[64,512]{1,0:T(8,128)S(1)}, f32[64,512]{1,0:T(8,128)S(1)}, u32[]{:S(2)}, u32[]{:S(2)}) collective-permute-start(f32[64,512]{1,0:T(8,128)S(1)} %copy-done.3), channel_id=1, source_target_pairs={{0,16},{4,20},{8,24},{12,28},{16,0},{20,4},{24,8},{28,12},{1,17},{... | collective-permute-start | bytes 393224 | tf_op jit(solution)/shard_map/ppermute | solution.py:426
  6.4 8.9 %collective-permute-start.5 = (f32[64,512]{1,0:T(8,128)S(1)}, f32[64,512]{1,0:T(8,128)S(1)}, u32[]{:S(2)}, u32[]{:S(2)}) collective-permute-start(f32[64,512]{1,0:T(8,128)S(1)} %copy-done.3), channel_id=1, source_target_pairs={{0,8},{4,12},{8,0},{12,4},{16,24},{20,28},{24,16},{28,20},{1,9},{5... | collective-permute-start | bytes 393224 | tf_op jit(solution)/shard_map/ppermute | solution.py:426
  7.0 8.4 %collective-permute-start.4 = (f32[64,512]{1,0:T(8,128)S(1)}, f32[64,512]{1,0:T(8,128)S(1)}, u32[]{:S(2)}, u32[]{:S(2)}) collective-permute-start(f32[64,512]{1,0:T(8,128)S(1)} %copy-done.3), channel_id=1, source_target_pairs={{0,4},{4,0},{8,12},{12,8},{16,20},{20,16},{24,28},{28,24},{1,5},{5... | collective-permute-start | bytes 393224 | tf_op jit(solution)/shard_map/ppermute | solution.py:426
  7.0 9.0 %collective-permute-start.9 = (f32[64,512]{1,0:T(8,128)S(1)}, f32[64,512]{1,0:T(8,128)S(1)}, u32[]{:S(2)}, u32[]{:S(2)}) collective-permute-start(f32[64,512]{1,0:T(8,128)S(1)} %copy-done.3), channel_id=1, source_target_pairs={{0,24},{4,28},{8,16},{12,20},{16,8},{20,12},{24,0},{28,4},{1,25},{... | collective-permute-start | bytes 393224 | tf_op jit(solution)/shard_map/ppermute | solution.py:426
  10.1 7.3 %copy-start.4 = (s32[1024]{0:T(1024)S(1)}, s32[1024]{0:T(1024)}, u32[]{:S(2)}) copy-start(s32[1024]{0:T(1024)} %param.11) | copy-start | bytes 12292
  10.1 7.3 %copy-start.5 = (s32[1024,1]{0,1:T(1,128)S(1)}, s32[1024,1]{0,1:T(1,128)}, u32[]{:S(2)}) copy-start(s32[1024,1]{0,1:T(1,128)} %param.10) | copy-start | bytes 12292
  10.2 12.6 %collective-permute-start.2 = (f32[40,8,128]{2,1,0:T(8,128)S(1)}, f32[40,8,128]{2,1,0:T(8,128)S(1)}, u32[]{:S(2)}, u32[]{:S(2)}) collective-permute-start(f32[40,8,128]{2,1,0:T(8,128)S(1)} %get-tuple-element.15), channel_id=1, source_target_pairs={{0,1},{1,2},{2,3},{3,0},{4,5},{5,6},{6,7},{7,4},{8,9},{9,10},{10,1... | collective-permute-start | bytes 491528 | tf_op jit(solution)/shard_map/ppermute | solution.py:437
  11.8 11.0 %collective-permute-start.3 = (f32[40,8,128]{2,1,0:T(8,128)S(1)}, f32[40,8,128]{2,1,0:T(8,128)S(1)}, u32[]{:S(2)}, u32[]{:S(2)}) collective-permute-start(f32[40,8,128]{2,1,0:T(8,128)S(1)} %get-tuple-element.16), channel_id=1, source_target_pairs={{0,3},{1,0},{2,1},{3,2},{4,7},{5,4},{6,5},{7,6},{8,11},{9,8},{10,9... | collective-permute-start | bytes 491528 | tf_op jit(solution)/shard_map/ppermute | solution.py:438
  15.4 1.3 %collective-permute-start.8 = (f32[64,512]{1,0:T(8,128)S(1)}, f32[64,512]{1,0:T(8,128)S(1)}, u32[]{:S(2)}, u32[]{:S(2)}) collective-permute-start(f32[64,512]{1,0:T(8,128)S(1)} %collective-permute-done.7.refs_4_), channel_id=1, source_target_pairs={{0,4},{4,0},{8,12},{12,8},{16,20},{20,16},{24,28},{28,24},{1,5},{5... | collective-permute-start | bytes 393224 | tf_op jit(solution)/shard_map/ppermute | solution.py:426
  15.4 1.5 %collective-permute-start.6 = (f32[64,512]{1,0:T(8,128)S(1)}, f32[64,512]{1,0:T(8,128)S(1)}, u32[]{:S(2)}, u32[]{:S(2)}) collective-permute-start(f32[64,512]{1,0:T(8,128)S(1)} %collective-permute-done.5.refs_2_), channel_id=1, source_target_pairs={{0,4},{4,0},{8,12},{12,8},{16,20},{20,16},{24,28},{28,24},{1,5},{5... | collective-permute-start | bytes 393224 | tf_op jit(solution)/shard_map/ppermute | solution.py:426
  16.0 1.3 %collective-permute-start.10 = (f32[64,512]{1,0:T(8,128)S(1)}, f32[64,512]{1,0:T(8,128)S(1)}, u32[]{:S(2)}, u32[]{:S(2)}) collective-permute-start(f32[64,512]{1,0:T(8,128)S(1)} %collective-permute-done.9.refs_6_), channel_id=1, source_target_pairs={{0,4},{4,0},{8,12},{12,8},{16,20},{20,16},{24,28},{28,24},{1,5},{5... | collective-permute-start | bytes 393224 | tf_op jit(solution)/shard_map/ppermute | solution.py:426
  19.0 5.2 %collective-permute-start.12 = (f32[1,1280]{1,0:T(1,128)S(1)}, f32[1,1280]{1,0:T(1,128)S(1)}, u32[]{:S(2)}, u32[]{:S(2)}) collective-permute-start(f32[1,1280]{1,0:T(1,128)S(1)} %sources.1.own), channel_id=1, source_target_pairs={{0,3},{1,0},{2,1},{3,2},{4,7},{5,4},{6,5},{7,6},{8,11},{9,8},{10,9... | collective-permute-start | bytes 15368 | tf_op jit(solution)/shard_map/ppermute | solution.py:441
  22.8 5.4 %collective-permute-start.11 = (f32[1,1280]{1,0:T(1,128)S(1)}, f32[1,1280]{1,0:T(1,128)S(1)}, u32[]{:S(2)}, u32[]{:S(2)}) collective-permute-start(f32[1,1280]{1,0:T(1,128)S(1)} %sources.1.own), channel_id=1, source_target_pairs={{0,1},{1,2},{2,3},{3,0},{4,5},{5,6},{6,7},{7,4},{8,9},{9,10},{10,1... | collective-permute-start | bytes 15368 | tf_op jit(solution)/shard_map/ppermute | solution.py:440

commit v4 on v2

v4 whole, which is shorter than its diff:
```python
import functools

import jax
import jax.numpy as jnp
from jax import lax
from jax.experimental import pallas as pl
from jax.experimental.pallas import tpu as pltpu
from jax.sharding import PartitionSpec as P

ITERS = 3
HALO = ITERS + 1
MOMENTS = 2 * ITERS
PAD = 8
BOTH = ("fluid", "solid")
VMEM = pl.BlockSpec(memory_space=pltpu.VMEM)
F32 = jnp.float32
BF16 = jnp.bfloat16


def params():
    return pltpu.CompilerParams(vmem_limit_bytes=24 * 1024 * 1024)


def cost(flops, size=0):
    return pl.CostEstimate(flops=flops, bytes_accessed=size, transcendentals=0)


def shift(axis, step):
    size = lax.axis_size(axis)
    return [(i, (i + step) % size) for i in range(size)]


def even():
    return lax.rem(lax.axis_index("fluid"), 2) == 0


def edge_kernel(field, inertia, flat, flat_inertia, factors, slot, holder, *refs):
    near, far, far_rows, first, last, marks, sems, side_sems = refs
    cx, cy, _ = field.shape
    thin = HALO - 1
    edge, thick = HALO * cy, thin * cy
    quads, rows = factors.shape
    top = edge + thick
    is_even = even()
    copies = []
    parts = ((near, near.at[top : top + quads, :]), (far, far_rows.at[0:quads, :]))
    for i, (out, out_rows) in enumerate(parts):
        at_end = is_even if i == 0 else jnp.logical_not(is_even)
        row = pl.multiple_of(jnp.where(at_end, rows - edge, 0), 128)
        cell = pl.multiple_of(jnp.where(at_end, rows - thick, 0), 8)
        pieces = (
            (flat.at[pl.ds(row, edge), :], out.at[0:edge, :]),
            (flat_inertia.at[pl.ds(cell, thick), :], out.at[edge:top, :]),
            (factors.at[:, pl.ds(row, edge)], out_rows),
            (slot.at[:, pl.ds(row, edge)], marks.at[2 * i]),
            (holder.at[:, pl.ds(row, edge)], marks.at[2 * i + 1]),
        )
        for j, (source, target) in enumerate(pieces):
            copies.append(pltpu.make_async_copy(source, target, sems.at[i, j]))
    for i, (out, at, inertia_at) in enumerate(((first, 0, 0), (last, cy - HALO, cy - thin))):
        pieces = (
            (field.at[:, at : at + HALO, :], out.at[:, 0:HALO, :]),
            (inertia.at[:, inertia_at : inertia_at + thin, :], out.at[:, HALO : HALO + thin, :]),
        )
        for j, (source, target) in enumerate(pieces):
            copies.append(pltpu.make_async_copy(source, target, side_sems.at[i, j]))
    for copy in copies:
        copy.start()
    for out in (first, last):
        out[:, HALO + thin : 2 * HALO, :] = jnp.zeros((cx, 1, out.shape[2]), F32)
    for copy in copies:
        copy.wait()
    for i, (out, at) in enumerate(((near, top + quads), (far_rows, quads))):
        packed = [marks[2 * i].astype(F32), marks[2 * i + 1].astype(F32), jnp.zeros((6, edge), F32)]
        out[at : at + 8, :] = jnp.concatenate(packed, axis=0)


def edges(field, inertia, factors, slot, holder):
    cx, cy, cz = field.shape
    thin = HALO - 1
    edge = HALO * cy
    layers, rows = edge + thin * cy, factors.shape[0] + 8
    flat, flat_inertia = field.reshape(cx * cy, cz), inertia.reshape(cx * cy, cz)
    operands = (field, inertia, flat, flat_inertia, factors, slot, holder)
    shapes = ((layers + rows, cz), (layers, cz), (rows, cz)) + ((cx, 2 * HALO, cz),) * 2
    return pl.pallas_call(
        edge_kernel,
        out_shape=tuple(jax.ShapeDtypeStruct(shape, F32) for shape in shapes),
        in_specs=[pl.BlockSpec(memory_space=pltpu.HBM)] * len(operands),
        out_specs=(VMEM,) * len(shapes),
        scratch_shapes=[
            pltpu.VMEM((4, 1, edge), jnp.int32),
            pltpu.SemaphoreType.DMA((2, 5)),
            pltpu.SemaphoreType.DMA((2, 2)),
        ],
        compiler_params=params(),
        cost_estimate=cost(10**5),
        name="edges",
    )(*(pltpu.with_memory_space_constraint(t, pltpu.HBM) for t in operands))


def source_kernel(count, cy, *refs):
    blocks = refs[:count]
    factors, slot, holder, near, far, far_rows, to_left, to_right, table, picked, out = refs[count:]
    quads, faces = blocks[0].shape
    rows = factors.shape[1]
    cz = near.shape[1]
    thin = HALO - 1
    edge, thick = HALO * cy, thin * cy
    top = edge + thick
    me = lax.axis_index("fluid")
    for k in range(count):
        value = blocks[k][...]
        high = value.astype(BF16)
        low = (value - high.astype(F32)).astype(BF16)
        table[2 * k * quads : (2 * k + 1) * quads, :] = high
        table[(2 * k + 1) * quads : (2 * k + 2) * quads, :] = low

    def part(slots, holders, weights, width):
        spot = lax.broadcasted_iota(jnp.int32, (faces, width), 0)
        chosen = jnp.where(spot == slots, 1.0, 0.0).astype(BF16)
        picked[:, 0:width] = jnp.dot(table[...], chosen, preferred_element_type=F32)
        total = jnp.zeros((quads, width), F32)
        for k in range(count):
            high = picked[2 * k * quads : (2 * k + 1) * quads, 0:width]
            low = picked[(2 * k + 1) * quads : (2 * k + 2) * quads, 0:width]
            total = total + jnp.where(holders == (me ^ k), high + low, 0.0)
        return jnp.sum(total * weights, axis=0, keepdims=True)

    is_even = even()

    def side(one, other):
        got = jnp.where(is_even, one[...], other[...])
        marks = got[quads : quads + 8].astype(jnp.int32)
        return marks[0:1], marks[1:2], got[0:quads]

    near_rows = near.at[top : top + quads + 8, :]
    parts = zip(side(far_rows, near_rows), side(near_rows, far_rows))
    slots, holders, weights = (jnp.concatenate(t, axis=1) for t in parts)
    both = part(slots, holders, weights, 2 * edge)
    out[:, 0:edge] = both[:, 0:edge]
    out[:, edge + rows : 2 * edge + rows] = both[:, edge : 2 * edge]
    width = 2 * edge
    for at in range(0, rows, width):
        spots = slice(at, at + width)
        out[:, edge + at : edge + at + width] = part(slot[:, spots], holder[:, spots], factors[:, spots], width)

    strips = 2 * thin * 2 * HALO
    for target, field_at, inertia_at in ((to_left, 0, 0), (to_right, cy - HALO, cy - thin)):
        for i in range(2 * thin):
            x = i + 1 if i < thin else i - thin
            one, other = (far, near) if i < thin else (near, far)
            at = x * cy + field_at
            strip = [jnp.where(is_even, one[at : at + HALO, :], other[at : at + HALO, :])]
            at = edge + (i % thin) * cy + inertia_at
            strip.append(jnp.where(is_even, one[at : at + thin, :], other[at : at + thin, :]))
            strip.append(jnp.zeros((1, cz), F32))
            target[2 * HALO * i : 2 * HALO * (i + 1), :] = jnp.concatenate(strip, axis=0)
        lines = [out[:, at : at + cz] for at in range(0, rows + 2 * edge, cz)]
        spare = target.shape[0] - strips - len(lines)
        lines.append(jnp.zeros((spare, cz), F32))
        target[strips:, :] = jnp.concatenate(lines, axis=0)


def source_lines(rows, edge, cz):
    return -(-(rows + 2 * edge) // (8 * cz)) * 8


def sources(blocks, factors, slot, holder, near, far, far_rows, cy):
    count = len(blocks)
    quads, rows = factors.shape
    faces = blocks[0].shape[1]
    edge = HALO * cy
    cz = near.shape[1]
    length = 4 * HALO * (HALO - 1) + source_lines(rows, edge, cz)
    shape = jax.ShapeDtypeStruct((length, cz), F32)
    return pl.pallas_call(
        functools.partial(source_kernel, count, cy),
        out_shape=(shape, shape),
        in_specs=[VMEM] * (count + 6),
        out_specs=(VMEM, VMEM),
        scratch_shapes=[
            pltpu.VMEM((2 * quads * count, faces), BF16),
            pltpu.VMEM((2 * quads * count, 2 * edge), F32),
            pltpu.VMEM((1, rows + 2 * edge), F32),
        ],
        compiler_params=params(),
        cost_estimate=cost(10**8),
        name="sources",
    )(*blocks, factors, slot, holder, near, far, far_rows)


def neighbours(ref, at, wide, before, centre, after):
    lane = lax.broadcasted_iota(jnp.int32, centre.shape, 1)
    depth = centre.shape[1]
    lower = jnp.where(lane == 0, 0.0, pltpu.roll(centre, 1, 1))
    upper = jnp.where(lane == depth - 1, 0.0, pltpu.roll(centre, depth - 1, 1))
    total = before + after
    total = total + (ref[at - 1 : at - 1 + wide, :] + ref[at + 1 : at + 1 + wide, :])
    return total + (lower + upper)


def sweep(ref, wide, low, high, out):
    def plane(x):
        return ref[PAD + x * wide : PAD + (x + 1) * wide, :]

    before, centre = plane(low - 1), plane(low)
    for x in range(low, high):
        after = plane(x + 1)
        out(x, neighbours(ref, PAD + x * wide, wide, before, centre, after), centre)
        before, centre = centre, after


def clear(ref, low, high):
    ref[low:high, :] = jnp.zeros((high - low, ref.shape[1]), F32)


def widen_kernel(field, inertia, left, right, wide_field, inverse, misfit):
    cx, cy, cz = field.shape
    thin = HALO - 1
    wide = cy + 2 * HALO
    j = lax.axis_index("solid")
    has_left, has_right = j > 0, j < lax.axis_size("solid") - 1
    clear(wide_field, 0, PAD)
    clear(wide_field, PAD + cx * wide, 2 * PAD + cx * wide)
    for x in range(cx):
        before = jnp.where(has_left, left[x], 0.0)
        after = jnp.where(has_right, right[x], 0.0)
        here = slice(PAD + x * wide, PAD + (x + 1) * wide)
        wide_field[here, :], inverse[here, :] = layer(before, field[x], inertia[x], after)

    def put(x, total, centre):
        misfit[PAD + x * wide : PAD + (x + 1) * wide, :] = total - 6.0 * centre

    sweep(wide_field, wide, 1, cx - 1, put)


def layer(before, middle, capacity, after):
    thin = HALO - 1
    none = jnp.zeros((1, middle.shape[1]), F32)
    values = jnp.concatenate([before[0:HALO], middle, after[0:HALO]], axis=0)
    full = [none, before[HALO : HALO + thin], capacity, after[HALO : HALO + thin], none]
    full = jnp.concatenate(full, axis=0)
    return values, jnp.where(full > 0.0, 1.0 / (6.0 + full), 0.0)


def widen(field, inertia, left, right):
    cx, cy, cz = field.shape
    shape = jax.ShapeDtypeStruct((cx * (cy + 2 * HALO) + 2 * PAD, cz), F32)
    return pl.pallas_call(
        widen_kernel,
        out_shape=(shape,) * 3,
        in_specs=[VMEM] * 4,
        out_specs=(VMEM,) * 3,
        compiler_params=params(),
        cost_estimate=cost(10**7),
        name="widen",
    )(field, inertia, left, right)


def basis_kernel(devices, inertia, near, far, wide_field, inverse, misfit, own, left, right, *outs):
    basis, sums = outs[: ITERS + 1], outs[ITERS + 1]
    spread, below_field, above_field, ends, end_inverse = outs[ITERS + 2 :]
    cx, cy, cz = inertia.shape
    thin = HALO - 1
    edge = HALO * cy
    wide = cy + 2 * HALO
    tall = cx + 2 * HALO
    strips = 2 * thin * 2 * HALO

    is_even = even()
    i, j = lax.axis_index("fluid"), lax.axis_index("solid")
    has_below, has_above = i > 0, i < lax.axis_size("fluid") - 1
    has_left, has_right = j > 0, j < lax.axis_size("solid") - 1

    def ends_of(one, other, low, high):
        return jnp.where(is_even, one[low:high, :], other[low:high, :])

    def rows_at(x):
        return slice(PAD + x * wide, PAD + (x + 1) * wide)

    none = jnp.zeros((2 * HALO, cz), F32)
    blank = jnp.zeros((cy, cz), F32)
    for upper, ref, inside in ((False, below_field, has_below), (True, above_field, has_above)):
        one, other = (near, far) if upper else (far, near)
        clear(ref, 0, PAD)
        clear(ref, PAD + (HALO + 2) * wide, 2 * PAD + (HALO + 2) * wide)
        for x in range(HALO):
            middle = ends_of(one, other, x * cy, (x + 1) * cy)
            outer = x == (thin if upper else 0)
            at = x if upper else x - 1
            if outer:
                capacity, before, after = blank, none, none
            else:
                capacity = ends_of(one, other, edge + at * cy, edge + (at + 1) * cy)
                line = 2 * HALO * (at + (thin if upper else 0))
                before, after = left[line : line + 2 * HALO, :], right[line : line + 2 * HALO, :]
                before, after = jnp.where(has_left, before, 0.0), jnp.where(has_right, after, 0.0)
            parts = [jnp.where(inside, t, 0.0) for t in (before, middle, capacity, after)]
            values, inverted = layer(*parts)
            ref[rows_at(x + 2 if upper else x), :] = values
            end_inverse[rows_at(x + HALO if upper else x), :] = inverted
        for x in range(2):
            at = cx - 2 + x if upper else x
            ref[rows_at(x if upper else x + HALO), :] = wide_field[rows_at(at), :]

    def put_below(x, total, centre):
        ends[rows_at(x), :] = total - 6.0 * centre

    sweep(below_field, wide, 1, HALO + 1, put_below)

    def put_above(x, total, centre):
        ends[rows_at(x + HALO), :] = total - 6.0 * centre

    sweep(above_field, wide, 1, HALO + 1, put_above)

    def misfit_at(x):
        if x <= HALO:
            return ends[rows_at(x), :]
        if x >= cx + HALO - 1:
            return ends[rows_at(x - cx + 2), :]
        return misfit[rows_at(x - HALO), :]

    def inverse_at(x):
        if x < HALO:
            return end_inverse[rows_at(x), :]
        if x >= cx + HALO:
            return end_inverse[rows_at(x - cx), :]
        return inverse[rows_at(x - HALO), :]

    def lines_of(ref):
        count = (cx + 2 * HALO) * cy // cz
        return jnp.concatenate([ref[strips + m : strips + m + 1, :] for m in range(count)], axis=1)

    rows = jnp.concatenate([lines_of(own), lines_of(left), lines_of(right)], axis=0)
    high = rows.astype(BF16)
    rest = rows - high.astype(F32)
    mid = rest.astype(BF16)
    low = (rest - mid.astype(F32)).astype(BF16)
    stack = jnp.concatenate([high.astype(F32), mid.astype(F32), low.astype(F32)], axis=0)
    index = lax.broadcasted_iota(jnp.int32, (9, cz), 0)
    lane9 = lax.broadcasted_iota(jnp.int32, (9, cz), 1)
    place = jnp.where(lane9 == cz - 1 - index % 3, 1.0, 0.0)
    spread[...] = lax.dot_general(
        stack.astype(BF16), place.astype(BF16), (((0,), (0,)), ((), ())), preferred_element_type=F32
    )

    def top(value, back):
        lane = lax.broadcasted_iota(jnp.int32, value.shape, 1)
        if back:
            value = pltpu.roll(value, back, 1)
        return jnp.where(lane == cz - 1, value, 0.0)

    for k in range(ITERS):
        low, high = PAD + (1 + k) * wide, PAD + (tall - 1 - k) * wide
        clear(basis[k], low - 8, low)
        clear(basis[k], high, high + 8)
    for x in range(1, tall - 1):
        given = spread[x * cy : (x + 1) * cy, :]
        extra = jnp.concatenate(
            [top(given[cy - 8 : cy], 1)[8 - HALO : 8], top(given, 0), top(given[0:8], 2)[0:HALO]], axis=0
        )
        basis[0][rows_at(x), :] = (misfit_at(x) + extra) * inverse_at(x)
    for k in range(1, ITERS + 1):

        def put(x, total, centre):
            basis[k][rows_at(x), :] = total * inverse_at(x)

        sweep(basis[k - 1], wide, 1 + k, tall - 1 - k, put)

    totals = [jnp.zeros((8, cz), F32) for _ in range(MOMENTS)]
    for x in range(cx):
        at = PAD + (x + HALO) * wide + HALO
        parts = [ref[at : at + cy, :] for ref in basis]
        diagonal = 6.0 + inertia[x]
        scaled = [diagonal * part for part in parts[:ITERS]]
        for m in range(MOMENTS):
            product = scaled[m // 2] * parts[m - m // 2]
            totals[m] = totals[m] + jnp.sum(product.reshape(cy // 8, 8, cz), axis=0)
    lines = [jnp.sum(total, axis=0, keepdims=True) for total in totals]
    lines = jnp.sum(jnp.concatenate(lines, axis=0), axis=1, keepdims=True)
    lane = lax.broadcasted_iota(jnp.int32, (MOMENTS, cz), 1)
    index = lax.broadcasted_iota(jnp.int32, (MOMENTS, cz), 0)
    line = jnp.sum(jnp.where(lane == index, lines, 0.0), axis=0, keepdims=True)
    sums[...] = jnp.broadcast_to(line, sums.shape)


def make_basis(inertia, near, far, widened, own, left, right, devices):
    cx, cy, cz = inertia.shape
    wide = cy + 2 * HALO

    def layers(count):
        return (count * wide + 2 * PAD, cz)

    shape = jax.ShapeDtypeStruct(layers(cx + 2 * HALO), F32)
    outs = (shape,) * (ITERS + 1) + (jax.ShapeDtypeStruct((devices, cz), F32),)
    scratch = ((cx + 2 * HALO) * cy, cz), layers(HALO + 2), layers(HALO + 2), layers(2 * HALO + 2), layers(2 * HALO)
    return pl.pallas_call(
        functools.partial(basis_kernel, devices),
        out_shape=outs,
        in_specs=[VMEM] * 9,
        out_specs=(VMEM,) * len(outs),
        scratch_shapes=[pltpu.VMEM(shape, F32) for shape in scratch],
        compiler_params=params(),
        cost_estimate=cost(10**7),
        name="basis",
    )(inertia, near, far, *widened, own, left, right)


def finish_kernel(field, inertia, sums, *refs):
    basis, (state, misfit) = refs[: ITERS + 1], refs[ITERS + 1 :]
    cx, cy, cz = field.shape
    wide = cy + 2 * HALO
    line = jnp.sum(sums[...], axis=0, keepdims=True)
    lane = lax.broadcasted_iota(jnp.int32, line.shape, 1)
    moment = [jnp.sum(jnp.where(lane == m, line, 0.0), axis=1, keepdims=True) for m in range(MOMENTS)]

    def product(a, b):
        total = None
        for m in range(len(a) + len(b) - 1):
            weight = None
            for i in range(len(a)):
                if 0 <= m - i < len(b):
                    term = a[i] * b[m - i]
                    weight = term if weight is None else weight + term
            term = weight * moment[m]
            total = term if total is None else total + term
        return total

    one = jnp.ones((1, 1), F32)
    zero = jnp.zeros((1, 1), F32)
    precond, course, guess = [one], [one], [zero] * ITERS
    norm = moment[0]
    for iteration in range(ITERS):
        image = [a - b for a, b in zip(course + [zero], [zero] + course)]
        multiplier = norm / product(course, image)
        guess = [g + multiplier * c for g, c in zip(guess, course + [zero] * ITERS)]
        precond = [a - multiplier * b for a, b in zip(precond + [zero] * 2, image)]
        if iteration + 1 < ITERS:
            following = product(precond, precond)
            ratio = following / norm
            course = [a + ratio * b for a, b in zip(precond, course + [zero])]
            norm = following
    guess = [jnp.broadcast_to(g, (1, cz)) for g in guess]
    precond = [jnp.broadcast_to(g, (1, cz)) for g in precond]

    for x in range(cx):
        at = PAD + (x + HALO) * wide + HALO
        parts = [ref[at : at + cy, :] for ref in basis]
        value = field[x]
        for g, part in zip(guess, parts):
            value = value + g * part
        state[x] = value
        rest = precond[0] * parts[0]
        for g, part in zip(precond[1:], parts[1:]):
            rest = rest + g * part
        misfit[x] = (6.0 + inertia[x]) * rest


def finish(field, inertia, sums, basis):
    shape = jax.ShapeDtypeStruct(field.shape, F32)
    return pl.pallas_call(
        finish_kernel,
        out_shape=(shape, shape),
        in_specs=[VMEM] * (3 + len(basis)),
        out_specs=(VMEM, VMEM),
        compiler_params=params(),
        cost_estimate=cost(10**6),
        name="finish",
    )(field, inertia, sums, *basis)


def per_device(field, inertia, current, factors, holder, slot):
    count = lax.axis_size("fluid")
    devices = count * lax.axis_size("solid")
    cy = field.shape[1]
    holder = holder.reshape(1, -1)
    slot = slot.reshape(1, -1)

    def swap(value, k):
        return lax.ppermute(value, "fluid", [(i, i ^ k) for i in range(count)])

    blocks = {0: current}
    for k in range(count - 2, 0, -2):
        blocks[k] = swap(current, k)
    near, far, far_rows, first, last = edges(field, inertia, factors, slot, holder)
    near = swap(near, 1)
    outside = [(i, (i + 2 * (i % 2) - 1) % count) for i in range(count)]
    far_rows = lax.ppermute(far_rows, "fluid", outside)
    far = lax.ppermute(far, "fluid", outside)
    up, down = shift("solid", 1), shift("solid", -1)
    left = lax.ppermute(last, "solid", up)
    right = lax.ppermute(first, "solid", down)
    for k in range(0, count, 2):
        blocks[k + 1] = swap(blocks[k], 1)
    blocks = [blocks[k] for k in range(count)]
    to_left, to_right = sources(blocks, factors, slot, holder, near, far, far_rows, cy)
    from_left = lax.ppermute(to_right, "solid", up)
    from_right = lax.ppermute(to_left, "solid", down)
    widened = widen(field, inertia, left, right)
    *basis, sums = make_basis(inertia, near, far, widened, to_left, from_left, from_right, devices)
    sums = lax.all_to_all(sums, BOTH, 0, 0, tiled=True)
    return finish(field, inertia, sums, basis)


def solution(mesh):
    return jax.shard_map(
        per_device,
        mesh=mesh,
        in_specs=(
            P("fluid", "solid", None),
            P("fluid", "solid", None),
            P(None, ("fluid", "solid")),
            P(None, ("fluid", "solid")),
            P(("fluid", "solid"), None),
            P(("fluid", "solid")),
        ),
        out_specs=(P("fluid", "solid", None), P("fluid", "solid", None)),
        check_vma=False,
    )
```

time: 49.2 us -> 43.2 us (0.88)
  waiting for transfers between devices: 2.06 us -> 7.87 us
  starting transfers between devices: 21.4 us -> 15.9 us
  local copies, waits for them, and re-layouts: 4.42 us -> 0.03 us
  blocking collectives: 14.3 us -> 11.9 us
  Pallas kernels: 5.88 us -> 6.64 us
    ppermute x8, starting transfers between devices: 9.57 us -> 4.18 us  [swap(): return lax.ppermute(value, 'fluid', [(i, i ^ k) for i in range(count)])]
    unnamed x20 -> x12, local copies, waits for them, and re-layouts: 4.42 us -> 0.03 us
    ppermute x8, waiting for transfers between devices: 1.34 us -> 5 us  [swap(): return lax.ppermute(value, 'fluid', [(i, i ^ k) for i in range(count)])]
    ppermute x4 -> x5, starting transfers between devices: 11 us -> 8.25 us  [the longest x1 3.81 us: per_device(): from_right = lax.ppermute(to_left, 'solid', down)]
    ppermute x1, starting transfers between devices: 0.79 us -> 3.43 us  [per_device(): far = lax.ppermute(far, 'fluid', outside)]
    all_to_all x1, blocking collectives: 14.3 us -> 11.9 us  [per_device(): sums = lax.all_to_all(sums, BOTH, 0, 0, tiled=True)]
    ppermute x4 -> x5, waiting for transfers between devices: 0.72 us -> 2.86 us  [the longest x1 1.16 us: per_device(): right = lax.ppermute(first, 'solid', down)]
    pallas_call x5 -> x4, Pallas kernels: 4.48 us -> 5.24 us  [the longest x1 1.93 us: make_basis(): pl.pallas_call(functools.partial(basis_kernel, devices), out_shape=outs,...]
  transfers between devices with their start and end apart: 13 -> 14, of which waited for: 5 -> 6; matrix products, arithmetic and copies ran while one was open for 0% -> 0% of each run, Pallas kernels for 5% -> 5%
where the time goes in v4:
time: 43.2 us; the launch traced here: 43 us
  starting transfers between devices  15.9 us (37%)
  blocking collectives  11.9 us (28%)
  waiting for transfers between devices  7.87 us (18%)
  Pallas kernels  6.64 us (15%)
  between operations  0.73 us (2%)
    all_to_all x1, blocking collectives, per_device(): sums = lax.all_to_all(sums, BOTH, 0, 0, tiled=True)  11.9 us
    ppermute x8, waiting for transfers between devices, swap(): return lax.ppermute(value, 'fluid', [(i, i ^ k) for i in range(count)])  5 us
    ppermute x8, starting transfers between devices, swap(): return lax.ppermute(value, 'fluid', [(i, i ^ k) for i in range(count)])  4.18 us
    ppermute x1, starting transfers between devices, per_device(): from_right = lax.ppermute(to_left, 'solid', down)  3.81 us
    ppermute x1, starting transfers between devices, per_device(): far = lax.ppermute(far, 'fluid', outside)  3.43 us
    ppermute x1, starting transfers between devices, per_device(): left = lax.ppermute(last, 'solid', up)  2.19 us
    ppermute x1, starting transfers between devices, per_device(): right = lax.ppermute(first, 'solid', down)  2.11 us
    pallas_call x1, Pallas kernels, make_basis(): pl.pallas_call(functools.partial(basis_kernel, devices), out_shape=outs,...  1.93 us
  transfers between devices with their start and end apart: 14, of which 6 were waited for; matrix products, arithmetic and copies ran while one was open for 0% of the time, Pallas kernels for 5%

profile of v4, /device:TPU:0, one launch (start us, length us, event | category | flops | bytes accessed | tf_op | source)
XLA Modules:
  0.0 43.0 jit_solution(1462758455757821033)
XLA Ops:
  0.6 0.0 copy-start.3
  0.6 0.0 copy-start.2
  0.6 1.3 %edges.1 = (f32[296,128]{1,0:T(8,128)S(1)}, f32[224,128]{1,0:T(8,128)S(1)}, f32[72,128]{1,0:T(8,128)S(1)}, f32[32,8,128]{2,1,0:T(8,128)S(1)}, f32[32,8,128]{2,1,0:T(8,128)S(1)}) custom-call(f32[32,32,128]{2,1,0:T(8,128)} %field.5, f32[32,32,128]{2,1,0:T(8,128)} %inertia.7, f32[1024,128]{1,0:T(8,128)} %bitcast.9, f32[1024,128]{1,0:T(8,128)} %bitcast.8, ...), custom_call_target="tpu_custom_call" | custom-call | flops 100000 | tf_op jit(solution)/shard_map/edges/pallas_call | solution.py:86
  2.0 0.0 copy-start.5
  2.0 0.0 copy-start.4
  2.0 3.4 %collective-permute-start.1 = (f32[224,128]{1,0:T(8,128)S(1)}, f32[224,128]{1,0:T(8,128)S(1)}, u32[]{:S(2)}, u32[]{:S(2)}) collective-permute-start(f32[224,128]{1,0:T(8,128)S(1)} %get-tuple-element.18), channel_id=1, source_target_pairs={{0,28},{4,8},{8,4},{12,16},{16,12},{20,24},{24,20},{28,0},{1,29},{... | collective-permute-start | bytes 344072 | tf_op jit(solution)/shard_map/ppermute | solution.py:490
  5.4 0.1 collective-permute-start.11
  5.5 0.0 copy-done.3
  5.5 2.2 %collective-permute-start.7 = (f32[64,512]{1,0:T(8,128)S(1)}, f32[64,512]{1,0:T(8,128)S(1)}, u32[]{:S(2)}, u32[]{:S(2)}) collective-permute-start(f32[64,512]{1,0:T(8,128)S(1)} %copy-done.3), channel_id=1, source_target_pairs={{0,16},{4,20},{8,24},{12,28},{16,0},{20,4},{24,8},{28,12},{1,17},{... | collective-permute-start | bytes 393224 | tf_op jit(solution)/shard_map/ppermute | solution.py:481
  7.7 0.6 %collective-permute-start.5 = (f32[64,512]{1,0:T(8,128)S(1)}, f32[64,512]{1,0:T(8,128)S(1)}, u32[]{:S(2)}, u32[]{:S(2)}) collective-permute-start(f32[64,512]{1,0:T(8,128)S(1)} %copy-done.3), channel_id=1, source_target_pairs={{0,8},{4,12},{8,0},{12,4},{16,24},{20,28},{24,16},{28,20},{1,9},{5... | collective-permute-start | bytes 393224 | tf_op jit(solution)/shard_map/ppermute | solution.py:481
  8.3 0.9 %collective-permute-start.9 = (f32[64,512]{1,0:T(8,128)S(1)}, f32[64,512]{1,0:T(8,128)S(1)}, u32[]{:S(2)}, u32[]{:S(2)}) collective-permute-start(f32[64,512]{1,0:T(8,128)S(1)} %copy-done.3), channel_id=1, source_target_pairs={{0,24},{4,28},{8,16},{12,20},{16,8},{20,12},{24,0},{28,4},{1,25},{... | collective-permute-start | bytes 393224 | tf_op jit(solution)/shard_map/ppermute | solution.py:481
  9.2 1.0 %collective-permute-done.11.refs_13_ = f32[72,128]{1,0:T(8,128)S(1)} collective-permute-done((f32[72,128]{1,0:T(8,128)S(1)}, f32[72,128]{1,0:T(8,128)S(1)}, u32[]{:S(2)}, u32[]{:S(2)}) %collective-permute-start.11) | collective-permute-done | bytes 36896 | tf_op jit(solution)/shard_map/ppermute | solution.py:489
  10.2 0.0 collective-permute-start
  10.2 0.0 collective-permute-done.1.refs_12_.far
  10.2 0.5 %collective-permute-start.4 = (f32[64,512]{1,0:T(8,128)S(1)}, f32[64,512]{1,0:T(8,128)S(1)}, u32[]{:S(2)}, u32[]{:S(2)}) collective-permute-start(f32[64,512]{1,0:T(8,128)S(1)} %copy-done.3), channel_id=1, source_target_pairs={{0,4},{4,0},{8,12},{12,8},{16,20},{20,16},{24,28},{28,24},{1,5},{5... | collective-permute-start | bytes 393224 | tf_op jit(solution)/shard_map/ppermute | solution.py:481
  10.7 1.2 %collective-permute-done.7.refs_4_ = f32[64,512]{1,0:T(8,128)S(1)} collective-permute-done((f32[64,512]{1,0:T(8,128)S(1)}, f32[64,512]{1,0:T(8,128)S(1)}, u32[]{:S(2)}, u32[]{:S(2)}) %collective-permute-start.7) | collective-permute-done | bytes 131104 | tf_op jit(solution)/shard_map/ppermute | solution.py:481
  11.9 0.0 collective-permute-start.8
  11.9 2.2 %collective-permute-done.5.refs_2_ = f32[64,512]{1,0:T(8,128)S(1)} collective-permute-done((f32[64,512]{1,0:T(8,128)S(1)}, f32[64,512]{1,0:T(8,128)S(1)}, u32[]{:S(2)}, u32[]{:S(2)}) %collective-permute-start.5) | collective-permute-done | bytes 131104 | tf_op jit(solution)/shard_map/ppermute | solution.py:481
  14.0 0.0 collective-permute-start.6
  14.0 1.6 %collective-permute-done.9.refs_6_ = f32[64,512]{1,0:T(8,128)S(1)} collective-permute-done((f32[64,512]{1,0:T(8,128)S(1)}, f32[64,512]{1,0:T(8,128)S(1)}, u32[]{:S(2)}, u32[]{:S(2)}) %collective-permute-start.9) | collective-permute-done | bytes 131104 | tf_op jit(solution)/shard_map/ppermute | solution.py:481
  15.7 0.0 collective-permute-start.10
  15.7 0.0 collective-permute-done.4.refs_1_
  15.7 2.2 %collective-permute-start.2 = (f32[32,8,128]{2,1,0:T(8,128)S(1)}, f32[32,8,128]{2,1,0:T(8,128)S(1)}, u32[]{:S(2)}, u32[]{:S(2)}) collective-permute-start(f32[32,8,128]{2,1,0:T(8,128)S(1)} %get-tuple-element.19), channel_id=1, source_target_pairs={{0,1},{1,2},{2,3},{3,0},{4,5},{5,6},{6,7},{7,4},{8,9},{9,10},{10,1... | collective-permute-start | bytes 393224 | tf_op jit(solution)/shard_map/ppermute | solution.py:492
  17.9 0.0 collective-permute-done.refs_11_.near
  17.9 0.0 copy-start
  17.9 0.0 copy-start.1
  17.9 2.1 %collective-permute-start.3 = (f32[32,8,128]{2,1,0:T(8,128)S(1)}, f32[32,8,128]{2,1,0:T(8,128)S(1)}, u32[]{:S(2)}, u32[]{:S(2)}) collective-permute-start(f32[32,8,128]{2,1,0:T(8,128)S(1)} %get-tuple-element.20), channel_id=1, source_target_pairs={{0,3},{1,0},{2,1},{3,2},{4,7},{5,4},{6,5},{7,6},{8,11},{9,8},{10,9... | collective-permute-start | bytes 393224 | tf_op jit(solution)/shard_map/ppermute | solution.py:493
  20.0 0.0 collective-permute-done.8.refs_5_
  20.0 0.0 collective-permute-done.6.refs_3_
  20.0 0.0 collective-permute-done.10.refs_7_
  20.0 0.0 copy-done.2
  20.0 0.0 copy-done.5
  20.0 0.0 copy-done.4
  20.0 1.6 %sources.1 = (f32[64,128]{1,0:T(8,128)S(1)}, f32[64,128]{1,0:T(8,128)S(1)}) custom-call(f32[64,512]{1,0:T(8,128)S(1)} %copy-done.3, f32[64,512]{1,0:T(8,128)S(1)} %collective-permute-done.4.refs_1_, f32[64,512]{1,0:T(8,128)S(1)} %collective-permute-done.5.refs_2_, f32[64,512]{1,0:T(8,128)S(1)} %collective-permute-done.6.refs_3_, ...), custom_call_target="tpu_custom_call" | custom-call | flops 100000000 | tf_op jit(solution)/shard_map/sources/pallas_call | solution.py:177
  21.6 0.1 collective-permute-start.12
  21.7 3.8 %collective-permute-start.13 = (f32[64,128]{1,0:T(8,128)S(1)}, f32[64,128]{1,0:T(8,128)S(1)}, u32[]{:S(2)}, u32[]{:S(2)}) collective-permute-start(f32[64,128]{1,0:T(8,128)S(1)} %get-tuple-element.25.own), channel_id=1, source_target_pairs={{0,3},{1,0},{2,1},{3,2},{4,7},{5,4},{6,5},{7,6},{8,11},{9,8},{10,9... | collective-permute-start | bytes 98312 | tf_op jit(solution)/shard_map/ppermute | solution.py:499
  25.5 0.0 collective-permute-done.2.left
  25.5 1.2 %collective-permute-done.3.right = f32[32,8,128]{2,1,0:T(8,128)S(1)} collective-permute-done((f32[32,8,128]{2,1,0:T(8,128)S(1)}, f32[32,8,128]{2,1,0:T(8,128)S(1)}, u32[]{:S(2)}, u32[]{:S(2)}) %collective-permute-start.3) | collective-permute-done | bytes 131104 | tf_op jit(solution)/shard_map/ppermute | solution.py:493
  26.7 0.0 copy-done
  26.7 0.0 copy-done.1
  26.7 0.4 widen.1
  27.1 0.7 %collective-permute-done.12.left = f32[64,128]{1,0:T(8,128)S(1)} collective-permute-done((f32[64,128]{1,0:T(8,128)S(1)}, f32[64,128]{1,0:T(8,128)S(1)}, u32[]{:S(2)}, u32[]{:S(2)}) %collective-permute-start.12) | collective-permute-done | bytes 32800 | tf_op jit(solution)/shard_map/ppermute | solution.py:498
  27.8 0.0 collective-permute-done.13.right
  27.8 1.9 %basis.1 = (f32[1616,128]{1,0:T(8,128)S(1)}, f32[1616,128]{1,0:T(8,128)S(1)}, f32[1616,128]{1,0:T(8,128)S(1)}, f32[1616,128]{1,0:T(8,128)S(1)}, f32[32,128]{1,0:T(8,128)S(1)}) custom-call(f32[32,32,128]{2,1,0:T(8,128)S(1)} %copy-done, f32[296,128]{1,0:T(8,128)S(1)} %collective-permute-done.refs_11_.near, f32[224,128]{1,0:T(8,128)S(1)} %collective-permute-done.1.refs_12_.far, ...), custom_call_target="tpu_custom_call" | custom-call | flops 10000000 | tf_op jit(solution)/shard_map/basis/pallas_call | solution.py:398
  29.7 11.9 %all_to_all.11 = f32[32,1,128]{2,1,0:T(1,128)S(1)} all-to-all(f32[32,1,128]{2,1,0:T(1,128)S(1)} %bitcast.15), channel_id=1, replica_groups=mesh['fluid'=8,'solid'=4] {'fluid','solid'}, dimensions={0} | all-to-all | bytes 32768 | tf_op jit(solution)/shard_map/all_to_all | solution.py:502
  41.7 1.4 %finish.1 = (f32[32,32,128]{2,1,0:T(8,128)}, f32[32,32,128]{2,1,0:T(8,128)}) custom-call(f32[32,32,128]{2,1,0:T(8,128)S(1)} %copy-done.1, f32[32,32,128]{2,1,0:T(8,128)S(1)} %copy-done, f32[32,128]{1,0:T(8,128)S(1)} %bitcast.10, f32[1616,128]{1,0:T(8,128)S(1)} %get-tuple-element.28.refs_0_, f32[1616,128]{1,0:T(8,128)S(1)} %get-tuple-element.29.refs_1_, ...), custom_call_target="tpu_custom_call" | custom-call | flops 1000000 | tf_op jit(solution)/shard_map/finish/pallas_call | solution.py:462
Async XLA Ops:
  0.6 4.9 %copy-start.3 = (f32[64,512]{1,0:T(8,128)S(1)}, f32[64,512]{1,0:T(8,128)}, u32[]{:S(2)}) copy-start(f32[64,512]{1,0:T(8,128)} %refs_0_.1) | copy-start | bytes 393220
  0.6 19.4 %copy-start.2 = (f32[64,1024]{1,0:T(8,128)S(1)}, f32[64,1024]{1,0:T(8,128)}, u32[]{:S(2)}) copy-start(f32[64,1024]{1,0:T(8,128)} %refs_8_.1) | copy-start | bytes 786436
  2.0 18.0 %copy-start.5 = (s32[1024,1]{0,1:T(1,128)S(1)}, s32[1024,1]{0,1:T(1,128)}, u32[]{:S(2)}) copy-start(s32[1024,1]{0,1:T(1,128)} %param.10) | copy-start | bytes 12292
  2.0 18.0 %copy-start.4 = (s32[1024]{0:T(1024)S(1)}, s32[1024]{0:T(1024)}, u32[]{:S(2)}) copy-start(s32[1024]{0:T(1024)} %param.11) | copy-start | bytes 12292
  2.0 8.2 %collective-permute-start.1 = (f32[224,128]{1,0:T(8,128)S(1)}, f32[224,128]{1,0:T(8,128)S(1)}, u32[]{:S(2)}, u32[]{:S(2)}) collective-permute-start(f32[224,128]{1,0:T(8,128)S(1)} %get-tuple-element.18), channel_id=1, source_target_pairs={{0,28},{4,8},{8,4},{12,16},{16,12},{20,24},{24,20},{28,0},{1,29},{... | collective-permute-start | bytes 344072 | tf_op jit(solution)/shard_map/ppermute | solution.py:490
  5.4 4.7 %collective-permute-start.11 = (f32[72,128]{1,0:T(8,128)S(1)}, f32[72,128]{1,0:T(8,128)S(1)}, u32[]{:S(2)}, u32[]{:S(2)}) collective-permute-start(f32[72,128]{1,0:T(8,128)S(1)} %get-tuple-element.24), channel_id=1, source_target_pairs={{0,28},{4,8},{8,4},{12,16},{16,12},{20,24},{24,20},{28,0},{1,29},{... | collective-permute-start | bytes 110600 | tf_op jit(solution)/shard_map/ppermute | solution.py:489
  5.5 6.4 %collective-permute-start.7 = (f32[64,512]{1,0:T(8,128)S(1)}, f32[64,512]{1,0:T(8,128)S(1)}, u32[]{:S(2)}, u32[]{:S(2)}) collective-permute-start(f32[64,512]{1,0:T(8,128)S(1)} %copy-done.3), channel_id=1, source_target_pairs={{0,16},{4,20},{8,24},{12,28},{16,0},{20,4},{24,8},{28,12},{1,17},{... | collective-permute-start | bytes 393224 | tf_op jit(solution)/shard_map/ppermute | solution.py:481
  7.7 6.3 %collective-permute-start.5 = (f32[64,512]{1,0:T(8,128)S(1)}, f32[64,512]{1,0:T(8,128)S(1)}, u32[]{:S(2)}, u32[]{:S(2)}) collective-permute-start(f32[64,512]{1,0:T(8,128)S(1)} %copy-done.3), channel_id=1, source_target_pairs={{0,8},{4,12},{8,0},{12,4},{16,24},{20,28},{24,16},{28,20},{1,9},{5... | collective-permute-start | bytes 393224 | tf_op jit(solution)/shard_map/ppermute | solution.py:481
  8.3 7.4 %collective-permute-start.9 = (f32[64,512]{1,0:T(8,128)S(1)}, f32[64,512]{1,0:T(8,128)S(1)}, u32[]{:S(2)}, u32[]{:S(2)}) collective-permute-start(f32[64,512]{1,0:T(8,128)S(1)} %copy-done.3), channel_id=1, source_target_pairs={{0,24},{4,28},{8,16},{12,20},{16,8},{20,12},{24,0},{28,4},{1,25},{... | collective-permute-start | bytes 393224 | tf_op jit(solution)/shard_map/ppermute | solution.py:481
  10.2 7.7 %collective-permute-start = (f32[296,128]{1,0:T(8,128)S(1)}, f32[296,128]{1,0:T(8,128)S(1)}, u32[]{:S(2)}, u32[]{:S(2)}) collective-permute-start(f32[296,128]{1,0:T(8,128)S(1)} %get-tuple-element.17), channel_id=1, source_target_pairs={{0,4},{4,0},{8,12},{12,8},{16,20},{20,16},{24,28},{28,24},{1,5},{5... | collective-permute-start | bytes 454664 | tf_op jit(solution)/shard_map/ppermute | solution.py:481
  10.2 5.5 %collective-permute-start.4 = (f32[64,512]{1,0:T(8,128)S(1)}, f32[64,512]{1,0:T(8,128)S(1)}, u32[]{:S(2)}, u32[]{:S(2)}) collective-permute-start(f32[64,512]{1,0:T(8,128)S(1)} %copy-done.3), channel_id=1, source_target_pairs={{0,4},{4,0},{8,12},{12,8},{16,20},{20,16},{24,28},{28,24},{1,5},{5... | collective-permute-start | bytes 393224 | tf_op jit(solution)/shard_map/ppermute | solution.py:481
  11.9 8.1 %collective-permute-start.8 = (f32[64,512]{1,0:T(8,128)S(1)}, f32[64,512]{1,0:T(8,128)S(1)}, u32[]{:S(2)}, u32[]{:S(2)}) collective-permute-start(f32[64,512]{1,0:T(8,128)S(1)} %collective-permute-done.7.refs_4_), channel_id=1, source_target_pairs={{0,4},{4,0},{8,12},{12,8},{16,20},{20,16},{24,28},{28,24},{1,5},{5... | collective-permute-start | bytes 393224 | tf_op jit(solution)/shard_map/ppermute | solution.py:481
  14.0 6.0 %collective-permute-start.6 = (f32[64,512]{1,0:T(8,128)S(1)}, f32[64,512]{1,0:T(8,128)S(1)}, u32[]{:S(2)}, u32[]{:S(2)}) collective-permute-start(f32[64,512]{1,0:T(8,128)S(1)} %collective-permute-done.5.refs_2_), channel_id=1, source_target_pairs={{0,4},{4,0},{8,12},{12,8},{16,20},{20,16},{24,28},{28,24},{1,5},{5... | collective-permute-start | bytes 393224 | tf_op jit(solution)/shard_map/ppermute | solution.py:481
  15.7 4.3 %collective-permute-start.10 = (f32[64,512]{1,0:T(8,128)S(1)}, f32[64,512]{1,0:T(8,128)S(1)}, u32[]{:S(2)}, u32[]{:S(2)}) collective-permute-start(f32[64,512]{1,0:T(8,128)S(1)} %collective-permute-done.9.refs_6_), channel_id=1, source_target_pairs={{0,4},{4,0},{8,12},{12,8},{16,20},{20,16},{24,28},{28,24},{1,5},{5... | collective-permute-start | bytes 393224 | tf_op jit(solution)/shard_map/ppermute | solution.py:481
  15.7 9.8 %collective-permute-start.2 = (f32[32,8,128]{2,1,0:T(8,128)S(1)}, f32[32,8,128]{2,1,0:T(8,128)S(1)}, u32[]{:S(2)}, u32[]{:S(2)}) collective-permute-start(f32[32,8,128]{2,1,0:T(8,128)S(1)} %get-tuple-element.19), channel_id=1, source_target_pairs={{0,1},{1,2},{2,3},{3,0},{4,5},{5,6},{6,7},{7,4},{8,9},{9,10},{10,1... | collective-permute-start | bytes 393224 | tf_op jit(solution)/shard_map/ppermute | solution.py:492
  17.9 8.8 %copy-start = (f32[32,32,128]{2,1,0:T(8,128)S(1)}, f32[32,32,128]{2,1,0:T(8,128)}, u32[]{:S(2)}) copy-start(f32[32,32,128]{2,1,0:T(8,128)} %inertia.7) | copy-start | bytes 1572868
  17.9 8.8 %copy-start.1 = (f32[32,32,128]{2,1,0:T(8,128)S(1)}, f32[32,32,128]{2,1,0:T(8,128)}, u32[]{:S(2)}) copy-start(f32[32,32,128]{2,1,0:T(8,128)} %field.5) | copy-start | bytes 1572868
  17.9 8.8 %collective-permute-start.3 = (f32[32,8,128]{2,1,0:T(8,128)S(1)}, f32[32,8,128]{2,1,0:T(8,128)S(1)}, u32[]{:S(2)}, u32[]{:S(2)}) collective-permute-start(f32[32,8,128]{2,1,0:T(8,128)S(1)} %get-tuple-element.20), channel_id=1, source_target_pairs={{0,3},{1,0},{2,1},{3,2},{4,7},{5,4},{6,5},{7,6},{8,11},{9,8},{10,9... | collective-permute-start | bytes 393224 | tf_op jit(solution)/shard_map/ppermute | solution.py:493
  21.6 6.2 %collective-permute-start.12 = (f32[64,128]{1,0:T(8,128)S(1)}, f32[64,128]{1,0:T(8,128)S(1)}, u32[]{:S(2)}, u32[]{:S(2)}) collective-permute-start(f32[64,128]{1,0:T(8,128)S(1)} %get-tuple-element.26), channel_id=1, source_target_pairs={{0,1},{1,2},{2,3},{3,0},{4,5},{5,6},{6,7},{7,4},{8,9},{9,10},{10,1... | collective-permute-start | bytes 98312 | tf_op jit(solution)/shard_map/ppermute | solution.py:498
  21.7 6.1 %collective-permute-start.13 = (f32[64,128]{1,0:T(8,128)S(1)}, f32[64,128]{1,0:T(8,128)S(1)}, u32[]{:S(2)}, u32[]{:S(2)}) collective-permute-start(f32[64,128]{1,0:T(8,128)S(1)} %get-tuple-element.25.own), channel_id=1, source_target_pairs={{0,3},{1,0},{2,1},{3,2},{4,7},{5,4},{6,5},{7,6},{8,11},{9,8},{10,9... | collective-permute-start | bytes 98312 | tf_op jit(solution)/shard_map/ppermute | solution.py:499
